TPU v7x, 128 devices: a whole 4x4x4 slice. The times are simulated.
128 devices in a mesh: head: 4 (over y_hi, core), seq: 32 (over x, z, y_lo).
Axes of the slice: x: 4, y: 4 (y_hi: 2, y_lo: 2; y = y_hi * 2 + y_lo), z: 4, core: 2. Of those that a mesh axis runs over, the one named last changes fastest.
Arguments:
- queries: bfloat16 [32768, 4096], P('seq', 'head'), may hold values from -6 to 6
- keys: bfloat16 [32768, 512], P('seq', 'head'), may hold values from -6 to 6
- values: bfloat16 [32768, 512], P('seq', 'head'), may hold values from -6 to 6
- vertical: int32 [32, 8], P('head'), may hold values from 0 to 255, as said below
- slash: int32 [32, 8], P('head'), may hold values from 1 to 28, as said below
Outputs:
- attended: bfloat16 [32768, 4096], P(('seq', 'head'))
Inputs may be any that keep to these rules, and one draw needn't show every extreme that they name: `vertical`: each row names 8 different blocks. Within each group of 8 consecutive rows, the different blocks named that lie in one slab (blocks s * 8 to s * 8 + 7) number at most 4, and exactly 4 in some slab. `slash`: each row names 8 different offsets.
All inputs are finite; a program needn't handle non-finite values.
Results may differ from a plain program's by a relative error of at most 0.0033.
Values may be sent and summed in bfloat16 or wider, within the bound.
A program may use at most 128 MiB of HBM per device.

v0:
```python
import functools
import math

import jax
import jax.numpy as jnp
from jax import lax
from jax.experimental import pallas as pl
from jax.experimental.pallas import tpu as pltpu
from jax.sharding import PartitionSpec as P

BLK = 128
LARGEST_OFFSET = 28
CAP = 4
NEG = -1e30
PIECES = 2
EARLY = 6
VALUE_STRIDE = 3
MESH = pl.DeviceIdType.MESH


def block_weights(q, own, row, index_ref, bias_ref, kt_ref, causal, listed, factor):
    scores = [jnp.where(causal, jnp.dot(q, kt_ref[own], preferred_element_type=jnp.float32), NEG)]
    for n in range(0, listed, 2):
        a, b = index_ref[row + n], index_ref[row + n + 1]
        pair = jnp.dot(
            q, jnp.concatenate([kt_ref[a], kt_ref[b]], axis=1), preferred_element_type=jnp.float32
        )
        scores.append(pair[:, :BLK] + bias_ref[row + n])
        scores.append(pair[:, BLK:] + bias_ref[row + n + 1])
    top = functools.reduce(jnp.maximum, scores)
    top = jnp.max(top, axis=1, keepdims=True) * factor
    total = None
    rounded = []
    for s in scores:
        w = jnp.exp2(s * factor - top)
        total = w if total is None else total + w
        rounded.append(w.astype(jnp.bfloat16))
    return rounded, jnp.sum(total, axis=1, keepdims=True)


def block_mix(own_weights, pair_weights, total, own, row, index_ref, v_ref, listed):
    mixed = jnp.dot(own_weights, v_ref[own], preferred_element_type=jnp.float32)
    for n in range(0, listed, 2):
        a, b = index_ref[row + n], index_ref[row + n + 1]
        mixed += jnp.dot(
            pair_weights(n),
            jnp.concatenate([v_ref[a], v_ref[b]], axis=0),
            preferred_element_type=jnp.float32,
        )
    return (mixed / total).astype(jnp.bfloat16)


def layer_kernel(
    slash_ref,
    vertical_ref,
    queries_ref,
    kt_ref,
    v_ref,
    out_ref,
    index_ref,
    bias_ref,
    rank_ref,
    used_ref,
    found_ref,
    pack_ref,
    q_ref,
    kt_buf,
    v_buf,
    staged,
    early_weights,
    early_total,
    held,
    packed,
    held_sem,
    load_sem,
    chain_send,
    chain_recv,
    cross_send,
    cross_recv,
    out_local,
    out_send,
    out_recv,
    *,
    blocks,
    listed,
    width,
    heads,
    slabs,
    groups,
):
    slab = lax.axis_index("seq")
    group = lax.axis_index("head")
    chain_len = slabs // 2
    place, side = slab // 2, slab % 2
    piece = blocks // PIECES
    bufs = (kt_buf, v_buf)
    has_next = place + 1 < chain_len

    whole_blocks = slabs * blocks
    reach = (LARGEST_OFFSET + blocks - 1) // blocks
    pack_at = reach // 2
    cap_piece = CAP // PIECES

    def part(kv, place_of, side_of, c, far):
        origin = place_of * 2 + side_of
        if far:
            first = pl.multiple_of(whole_blocks + origin * CAP + c * cap_piece, cap_piece)
            return bufs[kv].at[pl.ds(first, cap_piece)]
        first = pl.multiple_of(origin * blocks + c * piece, piece)
        return bufs[kv].at[pl.ds(first, piece)]

    def sent(ref, t, kv, c, far):
        if t == pack_at and far:
            return packed.at[kv, pl.ds(c * cap_piece, cap_piece)]
        return ref

    def chain(t, kv, c):
        ref = part(kv, place - t, side, c, chain_far(t + 1))
        return pltpu.make_async_remote_copy(
            sent(ref, t, kv, c, chain_far(t + 1)), ref, chain_send.at[t, kv, c], chain_recv.at[t, kv, c],
            device_id={"seq": slab + 2}, device_id_type=MESH,
        )

    def chain_in(t, kv, c):
        ref = part(kv, place - t, side, c, chain_far(t))
        return pltpu.make_async_remote_copy(
            ref, ref, chain_send.at[t - 1, kv, c], chain_recv.at[t - 1, kv, c],
            device_id={"seq": slab - 2}, device_id_type=MESH,
        )

    def cross(t, kv, c, sender):
        ref = part(kv, place - t, sender, c, cross_far(t, sender))
        return pltpu.make_async_remote_copy(
            sent(ref, t, kv, c, cross_far(t, sender)), ref, cross_send.at[t, kv, c], cross_recv.at[t, kv, c],
            device_id={"seq": place * 2 + 1 - side}, device_id_type=MESH,
        )

    def chain_far(t):
        return 2 * t > reach

    def cross_far(t, sender):
        return (2 * t - 1 if sender else 2 * t + 1) > reach

    def cross_runs(t, sender, this_side):
        if t == 0 and sender == 1:
            return None
        return (side == this_side) & (place >= t)

    own_first = pl.multiple_of(slab * blocks, blocks)
    loads = [
        pltpu.make_async_copy(src, buf.at[pl.ds(own_first, blocks)], load_sem.at[kv])
        for kv, (src, buf) in enumerate(((kt_ref, kt_buf), (v_ref, v_buf)))
    ]
    loads.append(pltpu.make_async_copy(queries_ref, q_ref, load_sem.at[2]))
    for load in loads:
        load.start()

    barrier = pltpu.get_barrier_semaphore()
    pl.semaphore_signal(
        barrier, 1, device_id={"seq": place * 2 + 1 - side}, device_id_type=MESH
    )
    for d in range(1, groups):
        pl.semaphore_signal(
            barrier, 1, device_id={"head": lax.rem(group + d, groups)}, device_id_type=MESH
        )

    @pl.when(has_next)
    def _():
        pl.semaphore_signal(barrier, 1, device_id={"seq": slab + 2}, device_id_type=MESH)

    @pl.when(place > 0)
    def _():
        pl.semaphore_signal(barrier, 1, device_id={"seq": slab - 2}, device_id_type=MESH)

    pl.semaphore_wait(
        barrier, groups + has_next.astype(jnp.int32) + (place > 0).astype(jnp.int32)
    )
    def start_cross(t, kv, c, packed):
        for sender in range(2):
            runs = cross_runs(t, sender, sender)
            if runs is not None and (t == pack_at and cross_far(t, sender)) == packed:

                @pl.when(runs)
                def _():
                    cross(t, kv, c, sender).start()

    def start_chain(t, kv, c, packed):
        if t < chain_len - 1 and (t == pack_at and chain_far(t + 1)) == packed:

            @pl.when((place >= t) & has_next)
            def _():
                chain(t, kv, c).start()

    def pass_on(t, kv, c):
        if t > 0:

            @pl.when(place >= t)
            def _():
                chain_in(t, kv, c).wait_recv()

        start_chain(t, kv, c, False)
        start_cross(t, kv, c, False)
        if t == pack_at and c == PIECES - 1:

            @pl.when(place >= t)
            def _():
                first = pl.multiple_of(((place - t) * 2 + side) * blocks, blocks)
                move = pltpu.make_async_copy(
                    bufs[kv].at[pl.ds(first, blocks)], held.at[kv], held_sem.at[kv]
                )
                move.start()
                move.wait()
                for k in range(CAP):
                    picked = held[kv, 0].astype(jnp.float32) * pack_ref[k * blocks]
                    for n in range(1, blocks):
                        picked += held[kv, n].astype(jnp.float32) * pack_ref[k * blocks + n]
                    packed[kv, k] = picked.astype(jnp.bfloat16)

            for each in range(PIECES):
                start_chain(t, kv, each, True)
                start_cross(t, kv, each, True)

    def wait_cross(kv):
        for t in range(chain_len):
            for c in range(PIECES):
                for sender in range(2):
                    runs = cross_runs(t, sender, 1 - sender)
                    if runs is not None:

                        @pl.when(runs)
                        def _():
                            cross(t, kv, c, sender).wait_recv()

    base = slab * blocks
    slashes, verticals = slash_ref.shape[1], vertical_ref.shape[1]

    def rank_block(block, rank):
        used = block < 0
        for head in range(heads):
            for n in range(verticals):
                used = used | (vertical_ref[head, n] == block)
        rank = jnp.where(block % blocks == 0, 0, rank)
        rank_ref[block] = rank
        used_ref[block] = used.astype(jnp.int32)
        return rank + used.astype(jnp.int32)

    def place_verticals(head, carry):
        for n in range(verticals):
            block = vertical_ref[head, n]
            far = whole_blocks + (block // blocks) * CAP + rank_ref[block]
            found_ref[head * verticals + n] = jnp.where(
                block >= (slab - reach) * blocks, block, far
            )
        return carry

    def list_blocks(step, carry):
        head, own = step // blocks, base + step % blocks
        reached = [own - slash_ref[head, n] for n in range(slashes)]
        for n, block in enumerate(reached):
            ok = block >= 0
            index_ref[step * listed + n] = jnp.where(ok, block, own)
            bias_ref[step * listed + n] = jnp.where(ok, 0.0, NEG)
        for n in range(verticals):
            block = vertical_ref[head, n]
            ok = block < own
            for other in reached:
                ok = ok & (block != other)
            found = found_ref[head * verticals + n]
            index_ref[step * listed + slashes + n] = jnp.where(ok, found, own)
            bias_ref[step * listed + slashes + n] = jnp.where(ok, 0.0, NEG)
        return carry

    lists = heads * blocks
    loads[0].wait()
    for c in range(PIECES):
        pass_on(0, 0, c)
    lax.fori_loop(0, whole_blocks, rank_block, jnp.int32(0))
    packed_first = jnp.maximum((place - pack_at) * 2 + side, 0) * blocks
    for k in range(CAP):
        for n in range(blocks):
            block = packed_first + n
            hit = (used_ref[block] == 1) & (rank_ref[block] == k)
            pack_ref[k * blocks + n] = jnp.where(hit, 1.0, 0.0)
    for t in range(1, chain_len):
        for c in range(PIECES):
            pass_on(t, 0, c)
        if t == 1:
            lax.fori_loop(0, heads, place_verticals, 0)
            lax.fori_loop(0, lists // 4, list_blocks, 0)
        if t == 2:
            lax.fori_loop(lists // 4, lists // 2, list_blocks, 0)
    loads[1].wait()
    for c in range(PIECES):
        pass_on(0, 1, c)
    lax.fori_loop(lists // 2, lists, list_blocks, 0)
    wait_cross(0)
    loads[2].wait()

    factor = math.log2(math.e) / math.sqrt(width)
    causal = lax.broadcasted_iota(jnp.int32, (BLK, BLK), 0) >= lax.broadcasted_iota(
        jnp.int32, (BLK, BLK), 1
    )
    share = blocks // groups
    share_rows = share * BLK

    def out_columns(group_of, head):
        return pl.ds(pl.multiple_of((group_of * heads + head) * width, width), width)

    def out_copy(head, r):
        owner = lax.rem(group + 1 + r, groups)
        return pltpu.make_async_remote_copy(
            staged.at[head, pl.ds(pl.multiple_of(owner * share_rows, share_rows), share_rows)],
            out_ref.at[:, out_columns(group, head)],
            out_send.at[head, r], out_recv.at[head, r],
            device_id={"head": owner}, device_id_type=MESH,
        )

    def out_in(head, r):
        sender = lax.rem(group + groups - 1 - r, groups)
        return pltpu.make_async_remote_copy(
            staged.at[head, pl.ds(0, share_rows)],
            out_ref.at[:, out_columns(sender, head)],
            out_send.at[head, r], out_recv.at[head, r],
            device_id={"head": sender}, device_id_type=MESH,
        )

    def out_own(head):
        return pltpu.make_async_copy(
            staged.at[head, pl.ds(pl.multiple_of(group * share_rows, share_rows), share_rows)],
            out_ref.at[:, out_columns(group, head)],
            out_local.at[head],
        )

    early = early_weights.shape[0]
    values_due = []
    for t in range(1, chain_len):
        each = [[(t, c)] for c in range(PIECES)]
        values_due += [sum(each, [])] if t == pack_at else each

    def owned_blocks(step):
        head, r = step // groups, step % groups
        owner = lax.rem(group + 1 + r, groups)
        columns = pl.ds(pl.multiple_of(head * width, width), width)
        for u in range(share):
            i = owner * share + u
            rows = pl.ds(pl.multiple_of(i * BLK, BLK), BLK)
            yield head, rows, columns, base + i, (head * blocks + i) * listed

    def send_share(step):
        head, r = step // groups, step % groups

        @pl.when(r < groups - 1)
        def _():
            out_copy(head, r).start()

        @pl.when(r == groups - 1)
        def _():
            out_own(head).start()

    def weigh_early(step, carry):
        for k, due in enumerate(values_due):

            @pl.when(step == min(VALUE_STRIDE * (k + 1), early * groups - 1))
            def _():
                for t, c in due:
                    pass_on(t, 1, c)

        for head, rows, columns, own, row in owned_blocks(step):
            rounded, total = block_weights(
                q_ref[rows, columns], own, row, index_ref, bias_ref, kt_buf, causal, listed, factor
            )
            for n, w in enumerate(rounded):
                early_weights[head, rows, n * BLK : (n + 1) * BLK] = w
            early_total[head, rows, :] = jnp.broadcast_to(total, (BLK, width))
        return carry

    def mix_early(step, carry):
        for head, rows, columns, own, row in owned_blocks(step):
            staged[head, rows, :] = block_mix(
                early_weights[head, rows, :BLK],
                lambda n: early_weights[head, rows, (n + 1) * BLK : (n + 3) * BLK],
                early_total[head, rows, :],
                own, row, index_ref, v_buf, listed,
            )
        send_share(step)
        return carry

    def one_share(step, carry):
        for head, rows, columns, own, row in owned_blocks(step):
            rounded, total = block_weights(
                q_ref[rows, columns], own, row, index_ref, bias_ref, kt_buf, causal, listed, factor
            )
            staged[head, rows, :] = block_mix(
                rounded[0],
                lambda n: jnp.concatenate([rounded[1 + n], rounded[2 + n]], axis=1),
                total,
                own, row, index_ref, v_buf, listed,
            )
        send_share(step)
        return carry

    lax.fori_loop(0, early * groups, weigh_early, 0)
    wait_cross(1)
    lax.fori_loop(0, early * groups, mix_early, 0)
    lax.fori_loop(early * groups, heads * groups, one_share, 0)

    for kv in range(2):
        for t in range(chain_len):
            for c in range(PIECES):
                if t < chain_len - 1:

                    @pl.when((place >= t) & has_next)
                    def _():
                        chain(t, kv, c).wait_send()

                for sender in range(2):
                    runs = cross_runs(t, sender, sender)
                    if runs is not None:

                        @pl.when(runs)
                        def _():
                            cross(t, kv, c, sender).wait_send()

    def finish(head, carry):
        out_own(head).wait()
        for r in range(groups - 1):
            out_copy(head, r).wait_send()
            out_in(head, r).wait_recv()
        return carry

    lax.fori_loop(0, heads, finish, 0)


def shards(queries, keys, values, vertical, slash):
    width = keys.shape[1]
    rows = queries.shape[0]
    blocks = rows // BLK
    heads = vertical.shape[0]
    slabs, groups = lax.axis_size("seq"), lax.axis_size("head")
    kt = jnp.swapaxes(keys.reshape(blocks, BLK, width), 1, 2)
    v = values.reshape(blocks, BLK, width)
    listed = slash.shape[1] + vertical.shape[1]
    early = min(EARLY, heads)
    dma = pltpu.SemaphoreType.DMA
    hops = (slabs // 2, 2, PIECES)
    smem, anywhere = pl.BlockSpec(memory_space=pltpu.SMEM), pl.BlockSpec(memory_space=pl.ANY)
    return pl.pallas_call(
        functools.partial(
            layer_kernel,
            blocks=blocks,
            listed=listed,
            width=width,
            heads=heads,
            slabs=slabs,
            groups=groups,
        ),
        in_specs=[smem, smem, anywhere, anywhere, anywhere],
        out_specs=anywhere,
        out_shape=jax.ShapeDtypeStruct((rows // groups, groups * heads * width), jnp.bfloat16),
        scratch_shapes=[
            pltpu.SMEM((heads * blocks * listed,), jnp.int32),
            pltpu.SMEM((heads * blocks * listed,), jnp.float32),
            pltpu.SMEM((slabs * blocks,), jnp.int32),
            pltpu.SMEM((slabs * blocks,), jnp.int32),
            pltpu.SMEM((vertical.size,), jnp.int32),
            pltpu.SMEM((CAP * blocks,), jnp.float32),
            pltpu.VMEM(queries.shape, jnp.bfloat16),
            pltpu.VMEM((slabs * (blocks + CAP), width, BLK), jnp.bfloat16),
            pltpu.VMEM((slabs * (blocks + CAP), BLK, width), jnp.bfloat16),
            pltpu.VMEM((heads, rows, width), jnp.bfloat16),
            pltpu.VMEM((early, rows, (listed + 1) * BLK), jnp.bfloat16),
            pltpu.VMEM((early, rows, width), jnp.float32),
            pltpu.VMEM((2, blocks, BLK, width), jnp.bfloat16),
            pltpu.VMEM((2, CAP, BLK, width), jnp.bfloat16),
            dma((2,)),
            dma((3,)),
            dma(hops),
            dma(hops),
            dma(hops),
            dma(hops),
            dma((heads,)),
            dma((heads, groups - 1)),
            dma((heads, groups - 1)),
        ],
        compiler_params=pltpu.CompilerParams(
            collective_id=0, has_side_effects=True, vmem_limit_bytes=62 * 1024 * 1024
        ),
    )(slash, vertical, queries, kt, v)


def solution(mesh):
    in_specs = (
        P("seq", "head"),
        P("seq", "head"),
        P("seq", "head"),
        P("head", None),
        P("head", None),
    )
    out_specs = P(("seq", "head"), None)
    return jax.shard_map(shards, mesh=mesh, in_specs=in_specs, out_specs=out_specs, check_vma=False)
```

profile of v0, /device:TPU:103, one launch (start us, length us, event | category | flops | bytes accessed | tf_op | source)
XLA Modules:
  0.0 169.6 jit_solution(895031583827156184)
XLA Ops:
  0.0 1.8 %copy.6 = bf16[8,128,128]{1,2,0:T(8,128)(2,1)} copy(bf16[8,128,128]{2,1,0:T(8,128)(2,1)} %bitcast.5) | data formatting | bytes 524288 | tf_op jit(solution)/shard_map/reshape | solution.py:440
  1.8 164.7 %shard_map.55 = bf16[256,4096]{1,0:T(8,128)(2,1)} custom-call(s32[8,8]{1,0:T(8,128)} %slash_ref.1, s32[8,8]{1,0:T(8,128)} %vertical_ref.1, bf16[1024,1024]{1,0:T(8,128)(2,1)} %queries_ref.1, bf16[8,128,128]{2,1,0:T(8,128)(2,1)} %bitcast.3, bf16[8,128,128]{2,1,0:T(8,128)(2,1)} %bitcast.4), custom_call_target="tpu_custom_call" | custom-call | tf_op jit(solution)/shard_map/pallas_call | solution.py:447
  166.5 3.1 %copy.8 = bf16[256,4096]{1,0:T(8,128)(2,1)} copy(bf16[256,4096]{1,0:T(8,128)(2,1)} %shard_map.55) | data formatting | bytes 4194304
where the time goes:
time: 170 us
  Pallas kernels  165 us (97%)
  local copies, waits for them, and re-layouts  4.92 us (3%)
    pallas_call x1, Pallas kernels, shards(): pl.pallas_call(functools.partial(layer_kernel, blocks=blocks, listed=list...  165 us

commit v1 on v0

v1 whole, which is shorter than its diff:
```python
import functools
import math

import jax
import jax.numpy as jnp
from jax import lax
from jax.experimental import pallas as pl
from jax.experimental.pallas import tpu as pltpu
from jax.sharding import PartitionSpec as P

BLK = 128
LARGEST_OFFSET = 28
CAP = 4
NEG = -1e30
SIDE = 4
NODES = SIDE * SIDE
REACH = 4
HALF = CAP // 2
MESH = pl.DeviceIdType.MESH

COPIES = {}
COPIES["zp"] = ((0, 1), (0, 0), "full")
COPIES["zm"] = ((0, -1), (0, 0), "full")
COPIES["xp"] = ((1, 0), (0, 0), "full")
COPIES["xm"] = ((-1, 0), (0, 0), "full")
COPIES["zm2"] = ((0, -1), (0, 1), "full")
COPIES["xm2"] = ((-1, 0), (1, 0), "full")
for d in (1, -1, 2):
    COPIES["xpA", d] = ((1, 0), (0, d), "A")
    COPIES["xmA", d] = ((-1, 0), (0, d), "A")
    COPIES["xmA2", d] = ((-1, 0), (1, d), "A")
    COPIES["zpB", d] = ((0, 1), (d, 0), "B")
    COPIES["zmB", d] = ((0, -1), (d, 0), "B")
    COPIES["zmB2", d] = ((0, -1), (d, 1), "B")
NAMES = list(COPIES)

THEN = {name: [] for name in NAMES}
THEN["zm"] = ["zm2", ("xpA", 1), ("xmA", 1)]
THEN["zm2"] = [("xpA", 2), ("xmA", 2)]
THEN["zp"] = [("xpA", -1), ("xmA", -1)]
THEN["xm"] = ["xm2", ("zpB", 1), ("zmB", 1)]
THEN["xm2"] = [("zpB", 2), ("zmB", 2)]
THEN["xp"] = [("zpB", -1), ("zmB", -1)]
for d in (1, -1, 2):
    THEN["xmA", d] = [("xmA2", d)]
    THEN["zmB", d] = [("zmB2", d)]

FIRST = ["xm", "zm", "xp"]
SECOND = ["xm2", "zm2", ("zmB", 1), ("xmA", 1), ("xpA", 1)]
LATER = [
    [("zmB", -1)],
    [("xmA", 2)],
    [("zmB", 2)],
    ["zp"],
    [("xpA", 2)],
    [("zmB2", 1)],
    [("xmA2", 1)],
    [("zmB2", -1)],
    [("xmA", -1)],
    [("zpB", 1), ("xpA", -1)],
    [("zmB2", 2), ("xmA2", 2)],
    [("zpB", -1)],
    [("zpB", 2), ("xmA2", -1)],
]


def attended(slot, weights_of, blocks_of, pairs):
    mixed = None
    for n in range(pairs):
        part = jnp.dot(weights_of(n), blocks_of(n), preferred_element_type=jnp.float32)
        mixed = part if mixed is None else mixed + part
    return mixed


def layer_kernel(
    slash_ref,
    vertical_ref,
    queries_ref,
    kt_ref,
    v_ref,
    out_ref,
    table_v,
    table_s,
    found_v,
    found_s,
    q_ref,
    own_ref,
    near,
    far,
    staged,
    mixed_ref,
    top_ref,
    total_ref,
    scores_0,
    scores_1,
    scores_2,
    scores_3,
    tops,
    load_sem,
    swap_send,
    swap_recv,
    table_sem,
    near_send,
    near_recv,
    unit_send,
    unit_recv,
    twin_send,
    twin_recv,
    out_local,
    out_send,
    out_recv,
    *,
    blocks,
    heads,
    width,
    listed,
):
    seq, head = lax.axis_index("seq"), lax.axis_index("head")
    node, low = seq // 2, seq % 2
    high, core = head // 2, head % 2
    x, z = node // SIDE, node % SIDE
    group, slab = 2 * high + low, 2 * node + core
    native = low == core
    scores = (scores_0, scores_1, scores_2, scores_3)
    half = blocks // 2

    def at(dx, dz):
        to = lax.rem(x + dx + SIDE, SIDE) * SIDE + lax.rem(z + dz + SIDE, SIDE)
        return {"seq": 2 * to + low}

    follower = {"seq": 2 * lax.rem(node + 1, NODES) + low}
    leader = {"seq": 2 * lax.rem(node + NODES - 1, NODES) + low}
    twin = {"head": 2 * high + 1 - core}
    counterpart = {"seq": 2 * node + core, "head": 2 * high + low}

    def owner_of(quarter):
        return {"seq": slab, "head": quarter}

    def worker_of(of_group):
        return {"seq": 2 * node + lax.rem(of_group, 2), "head": 2 * (of_group // 2) + low}

    sources = [slash_ref, vertical_ref, kt_ref, v_ref]
    targets = [table_v.at[0], table_v.at[1], own_ref.at[:, 0], own_ref.at[:, 1]]
    for i in range(blocks):
        rows = pl.ds(i * BLK, BLK)
        sources.append(queries_ref.at[rows])
        targets.append(q_ref.at[rows])

    def load(k):
        return pltpu.make_async_copy(sources[k], targets[k], load_sem.at[k])

    def swap(k):
        return pltpu.make_async_remote_copy(
            sources[k], targets[k], swap_send.at[k], swap_recv.at[k],
            device_id=counterpart, device_id_type=MESH,
        )

    def wait_input(k):
        @pl.when(native)
        def _():
            load(k).wait()

        @pl.when(jnp.logical_not(native))
        def _():
            swap(k).wait_recv()

    @pl.when(native)
    def _():
        for k in range(len(sources)):
            load(k).start()

    barrier = pltpu.get_barrier_semaphore()

    def greet(device):
        pl.semaphore_signal(barrier, 1, device_id=device, device_id_type=MESH)

    for device in (at(1, 0), at(-1, 0), at(0, 1), at(0, -1), follower, leader, twin):
        greet(device)
    for k in range(4):

        @pl.when(jnp.logical_not(native & (head == k)))
        def _():
            greet(owner_of(k))

        @pl.when(jnp.logical_not(native & (group == k)))
        def _():
            greet(worker_of(jnp.int32(k)))

    @pl.when(jnp.logical_not(native))
    def _():
        greet(counterpart)

    pl.semaphore_wait(barrier, 7 + 6 + 3 * (low - core) * (low - core))

    @pl.when(jnp.logical_not(native))
    def _():
        for k in range(len(sources)):
            swap(k).start()

    def near_copy(src, dst, k, device):
        return pltpu.make_async_remote_copy(
            src, dst, near_send.at[k], near_recv.at[k], device_id=device, device_id_type=MESH
        )

    def near_part(back, c):
        return near.at[pl.ds((REACH - back) * blocks + c * half, half)]

    def hop_one(c):
        return near_copy(own_ref.at[pl.ds(c * half, half)], near_part(2, c), c, follower)

    def hop_two(c):
        return near_copy(near_part(2, c), near_part(4, c), 2 + c, follower)

    def twin_one(c, from_own):
        src = own_ref.at[pl.ds(c * half, half)] if from_own else near_part(2, c)
        return near_copy(src, near_part(1, c), 4 + c, twin)

    def twin_two(c, back):
        return near_copy(near_part(back, c), near_part(3, c), 6 + c, twin)

    def unit(dx, dz, part, of_core):
        to = lax.rem(x + dx + SIDE, SIDE) * SIDE + lax.rem(z + dz + SIDE, SIDE)
        first = (of_core * NODES + to) * CAP
        if part == "full":
            return far.at[pl.ds(pl.multiple_of(first, CAP), CAP)]
        if part == "B":
            first = first + HALF
        return far.at[pl.ds(pl.multiple_of(first, HALF), HALF)]

    def arrives(name):
        (sx, sz), (dx, dz), part = COPIES[name]
        return dx - sx, dz - sz, part

    def send(name):
        (sx, sz), (dx, dz), part = COPIES[name]
        ref, k = unit(dx, dz, part, core), NAMES.index(name)
        return pltpu.make_async_remote_copy(
            ref, ref, unit_send.at[k], unit_recv.at[k], device_id=at(sx, sz), device_id_type=MESH
        )

    def receive(name):
        (sx, sz), _, _ = COPIES[name]
        ref, k = unit(*arrives(name), core), NAMES.index(name)
        return pltpu.make_async_remote_copy(
            ref, ref, unit_send.at[k], unit_recv.at[k], device_id=at(-sx, -sz), device_id_type=MESH
        )

    def share(name, of_core):
        ref = unit(0, 0, "full", of_core) if name == "own" else unit(*arrives(name), of_core)
        k = len(NAMES) if name == "own" else NAMES.index(name)
        return pltpu.make_async_remote_copy(
            ref, ref, twin_send.at[k], twin_recv.at[k], device_id=twin, device_id_type=MESH
        )

    def event(name):
        receive(name).wait_recv()
        for following in THEN[name]:
            send(following).start()
        share(name, core).start()

    wait_input(0)
    wait_input(1)
    to_scalars = pltpu.make_async_copy(table_v, table_s, table_sem.at[0])
    to_scalars.start()
    to_scalars.wait()

    def note_used(h, used):
        for n in range(listed):
            block = table_s[1, h, n] - slab * blocks
            used = tuple(u | (block == j).astype(jnp.int32) for j, u in enumerate(used))
        return used

    used = lax.fori_loop(0, heads, note_used, (jnp.int32(0),) * blocks)
    picked = [jnp.int32(0)] * CAP
    rank = jnp.int32(0)
    for j in range(blocks):
        picked = [jnp.where((used[j] == 1) & (rank == k), j, at_k) for k, at_k in enumerate(picked)]
        rank = rank + used[j]

    wait_input(2)
    wait_input(3)
    for c in (1, 0):
        hop_one(c).start()

    own_unit = pl.multiple_of((core * NODES + node) * CAP, CAP)
    for k in range(CAP):
        for kv in range(2):
            far[own_unit + k, kv] = own_ref[picked[k], kv]

    @pl.when(core == 0)
    def _():
        for c in range(2):
            twin_one(c, True).start()

    for name in ("xm", "zm", "xp"):
        send(name).start()
    share("own", core).start()
    for j in range(blocks):
        for kv in range(2):
            near[REACH * blocks + j, kv] = own_ref[j, kv]

    verticals = table_v[1]
    first_of = verticals // blocks * blocks
    seen = jnp.zeros_like(verticals)
    for h in range(heads):
        for n in range(listed):
            there = table_s[1, h, n] - first_of
            for j in range(blocks - 1):
                seen = seen | jnp.where(there == j, 1 << j, 0)
    before = verticals - first_of
    place = jnp.zeros_like(verticals)
    for j in range(blocks - 1):
        place = place + jnp.where((before > j) & (seen & (1 << j) != 0), 1, 0)
    of_slab = verticals // blocks
    found_v[...] = ((of_slab % 2) * NODES + of_slab // 2) * CAP + place
    to_found = pltpu.make_async_copy(found_v, found_s, table_sem.at[1])
    to_found.start()
    to_found.wait()

    for name in FIRST:
        event(name)
    for c in (1, 0):
        hop_one(c).wait_recv()
        if c == 1:
            hop_two(c).start()
        else:

            @pl.when(core == 1)
            def _():
                hop_two(c).start()

        @pl.when(core == 1)
        def _():
            twin_one(c, False).start()

        @pl.when(core == 0)
        def _():
            twin_two(c, 2).start()

    send("zp").start()
    for name in SECOND:
        event(name)

    @pl.when(core == 1)
    def _():
        for c in (1, 0):
            hop_two(c).wait_recv()
            twin_two(c, 4).start()

    @pl.when(core == 0)
    def _():
        hop_two(1).wait_recv()

    for c in range(2):
        twin_one(c, True).wait_recv()
        twin_two(c, 2).wait_recv()

    factor = math.log2(math.e) / math.sqrt(width)
    causal = lax.broadcasted_iota(jnp.int32, (BLK, BLK), 0) >= lax.broadcasted_iota(
        jnp.int32, (BLK, BLK), 1
    )
    steps = heads * blocks
    base = slab * blocks

    def query(i, h):
        return q_ref[
            pl.ds(pl.multiple_of(i * BLK, BLK), BLK), pl.ds(pl.multiple_of(h * width, width), width)
        ]

    def pair_scores(q, ref, a, b, bias_a, bias_b):
        pair = jnp.dot(
            q, jnp.concatenate([ref[a, 0], ref[b, 0]], axis=1), preferred_element_type=jnp.float32
        )
        return pair[:, :BLK] + bias_a, pair[:, BLK:] + bias_b

    def pair_mix(ref, a, b, wa, wb):
        return jnp.dot(
            jnp.concatenate([wa.astype(jnp.bfloat16), wb.astype(jnp.bfloat16)], axis=1),
            jnp.concatenate([ref[a, 1], ref[b, 1]], axis=0),
            preferred_element_type=jnp.float32,
        )

    def near_entry(i, h, n):
        offset = table_s[0, h, n]
        return REACH * blocks + i - offset, jnp.where(base + i >= offset, 0.0, NEG)

    def near_scores(step, u):
        i, h = step // heads, step % heads
        q = query(i, h)
        own = jnp.dot(q, near[REACH * blocks + i, 0], preferred_element_type=jnp.float32)
        own = jnp.where(causal, own, NEG)
        scores[u][:, :BLK] = own
        top = own
        for n in range(0, listed, 2):
            (a, bias_a), (b, bias_b) = near_entry(i, h, n), near_entry(i, h, n + 1)
            sa, sb = pair_scores(q, near, a, b, bias_a, bias_b)
            scores[u][:, (n + 1) * BLK : (n + 2) * BLK] = sa
            scores[u][:, (n + 2) * BLK : (n + 3) * BLK] = sb
            top = jnp.maximum(top, jnp.maximum(sa, sb))
        top = jnp.max(top, axis=1, keepdims=True) * factor
        top_ref[step] = jnp.broadcast_to(top, (BLK, width))

    def near_mix(step, u):
        i, h = step // heads, step % heads
        top = top_ref[step]

        def weight(n):
            return jnp.exp2(scores[u][:, n * BLK : (n + 1) * BLK] * factor - top)

        total = weight(0)
        mixed = jnp.dot(
            total.astype(jnp.bfloat16), near[REACH * blocks + i, 1], preferred_element_type=jnp.float32
        )
        for n in range(0, listed, 2):
            a, b = near_entry(i, h, n)[0], near_entry(i, h, n + 1)[0]
            wa, wb = weight(n + 1), weight(n + 2)
            total = total + (wa + wb)
            mixed = mixed + pair_mix(near, a, b, wa, wb)
        mixed_ref[step] = mixed
        total_ref[step] = jnp.broadcast_to(jnp.sum(total, axis=1, keepdims=True), (BLK, width))

    def row_block(k):
        late = k // half
        quarter = 2 * ((1 - late) * (1 - high) + late * high) + (k % half) // 2
        return 2 * quarter + k % 2

    def far_bias(own, h, block):
        gap = own - block
        ok = gap > 0
        for n in range(listed):
            ok = ok & (gap != table_s[0, h, n])
        return jnp.where(ok, 0.0, NEG)

    def far_scores(step, u):
        i, h = row_block(step // heads), step % heads
        q = query(i, h)
        top = None
        for n in range(0, listed, 2):
            bias = [far_bias(base + i, h, table_s[1, h, n + d]) for d in range(2)]
            sa, sb = pair_scores(q, far, found_s[h, n], found_s[h, n + 1], *bias)
            scores[u][:, n * BLK : (n + 1) * BLK] = sa
            scores[u][:, (n + 1) * BLK : (n + 2) * BLK] = sb
            both = jnp.maximum(sa, sb)
            top = both if top is None else jnp.maximum(top, both)
        top = jnp.max(top, axis=1, keepdims=True) * factor
        tops[u] = jnp.maximum(jnp.broadcast_to(top, (BLK, width)), top_ref[i * heads + h])

    def far_mix(step, u):
        i, h = row_block(step // heads), step % heads
        top, kept = tops[u], i * heads + h
        scale = jnp.exp2(top_ref[kept] - top)
        total, mixed = None, None
        for n in range(0, listed, 2):
            wa = jnp.exp2(scores[u][:, n * BLK : (n + 1) * BLK] * factor - top)
            wb = jnp.exp2(scores[u][:, (n + 1) * BLK : (n + 2) * BLK] * factor - top)
            total = wa + wb if total is None else total + (wa + wb)
            part = pair_mix(far, found_s[h, n], found_s[h, n + 1], wa, wb)
            mixed = part if mixed is None else mixed + part
        total = jnp.sum(total, axis=1, keepdims=True) + total_ref[kept] * scale
        mixed = mixed + mixed_ref[kept] * scale
        rows = pl.ds(pl.multiple_of(i * BLK, BLK), BLK)
        staged[rows, pl.ds(pl.multiple_of(h * width, width), width)] = (mixed / total).astype(jnp.bfloat16)

    columns = pl.ds(pl.multiple_of(group * heads * width, heads * width), heads * width)

    def out_copy(k):
        i = row_block(k)
        owner, n = i // 2, k % 2
        return pltpu.make_async_remote_copy(
            staged.at[pl.ds(pl.multiple_of(i * BLK, BLK), BLK)],
            out_ref.at[pl.ds(pl.multiple_of(n * BLK, BLK), BLK), columns],
            out_send.at[k], out_recv.at[group * 2 + n],
            device_id=owner_of(owner), device_id_type=MESH,
        )

    def out_keep(k):
        i = row_block(k)
        n = k % 2
        return pltpu.make_async_copy(
            staged.at[pl.ds(pl.multiple_of(i * BLK, BLK), BLK)],
            out_ref.at[pl.ds(pl.multiple_of(n * BLK, BLK), BLK), columns],
            out_local.at[n],
        )

    def kept_here(k):
        return native & (row_block(k) // 2 == head)

    def out_in(of_group, n):
        return pltpu.make_async_remote_copy(
            staged.at[pl.ds(0, BLK)],
            out_ref.at[pl.ds(n * BLK, BLK), pl.ds(of_group * heads * width, heads * width)],
            out_send.at[0], out_recv.at[of_group * 2 + n],
            device_id=worker_of(jnp.int32(of_group)), device_id_type=MESH,
        )

    def send_block(k):
        @pl.when(kept_here(k))
        def _():
            out_keep(k).start()

        @pl.when(jnp.logical_not(kept_here(k)))
        def _():
            out_copy(k).start()

    def near_loop(k, carry):
        for j, names in enumerate(LATER):

            @pl.when(k == j + 1)
            def _():
                for name in names:
                    event(name)

        first = 4 * k
        near_scores(first + 2, 2)
        near_mix(first, 0)
        near_scores(first + 3, 3)
        near_mix(first + 1, 1)
        near_scores(lax.rem(first + 4, steps), 0)
        near_mix(first + 2, 2)
        near_scores(lax.rem(first + 5, steps), 1)
        near_mix(first + 3, 3)
        return carry

    for i in range(blocks):
        wait_input(4 + i)
    near_scores(0, 0)
    near_scores(1, 1)
    lax.fori_loop(0, steps // 4, near_loop, 0)

    for name in NAMES:
        share(name, 1 - core).wait_recv()
    share("own", 1 - core).wait_recv()

    def far_loop(k, carry):
        first = 4 * k
        far_scores(first + 2, 2)
        far_mix(first, 0)
        far_scores(first + 3, 3)
        far_mix(first + 1, 1)
        far_scores(lax.rem(first + 4, steps), 0)
        far_mix(first + 2, 2)
        far_scores(lax.rem(first + 5, steps), 1)
        far_mix(first + 3, 3)

        @pl.when(k % 2 == 1)
        def _():
            send_block(k // 2)

        return carry

    far_scores(0, 0)
    far_scores(1, 1)
    lax.fori_loop(0, steps // 4, far_loop, 0)

    @pl.when(jnp.logical_not(native))
    def _():
        for k in range(len(sources)):
            swap(k).wait_send()

    for c in range(2):
        hop_one(c).wait_send()
        twin_one(c, True).wait_send()
        twin_two(c, 2).wait_send()
    hop_two(1).wait_send()

    @pl.when(core == 1)
    def _():
        hop_two(0).wait_send()

    for name in NAMES:
        send(name).wait_send()
        share(name, core).wait_send()
    share("own", core).wait_send()

    for k in range(blocks):

        @pl.when(kept_here(k))
        def _():
            out_keep(k).wait()

        @pl.when(jnp.logical_not(kept_here(k)))
        def _():
            out_copy(k).wait_send()

    for of_group in range(4):

        @pl.when(jnp.logical_not(native & (group == of_group)))
        def _():
            for n in range(2):
                out_in(of_group, n).wait_recv()


def shards(queries, keys, values, vertical, slash):
    width = keys.shape[1]
    rows = queries.shape[0]
    blocks = rows // BLK
    heads, listed = vertical.shape
    groups = lax.axis_size("head")
    kt = jnp.swapaxes(keys.reshape(blocks, BLK, width), 1, 2)
    v = values.reshape(blocks, BLK, width)
    dma = pltpu.SemaphoreType.DMA
    anywhere = pl.BlockSpec(memory_space=pl.ANY)
    bf16, f32 = jnp.bfloat16, jnp.float32
    inputs = 4 + blocks
    near_width = (listed + 1) * BLK
    return pl.pallas_call(
        functools.partial(layer_kernel, blocks=blocks, heads=heads, width=width, listed=listed),
        in_specs=[anywhere] * 5,
        out_specs=anywhere,
        out_shape=jax.ShapeDtypeStruct((rows // groups, groups * heads * width), bf16),
        scratch_shapes=[
            pltpu.VMEM((2, heads, listed), jnp.int32),
            pltpu.SMEM((2, heads, listed), jnp.int32),
            pltpu.VMEM((heads, listed), jnp.int32),
            pltpu.SMEM((heads, listed), jnp.int32),
            pltpu.VMEM(queries.shape, bf16),
            pltpu.VMEM((blocks, 2, BLK, width), bf16),
            pltpu.VMEM(((REACH + 1) * blocks, 2, BLK, width), bf16),
            pltpu.VMEM((2 * NODES * CAP, 2, BLK, width), bf16),
            pltpu.VMEM(queries.shape, bf16),
            pltpu.VMEM((heads * blocks, BLK, width), f32),
            pltpu.VMEM((heads * blocks, BLK, width), f32),
            pltpu.VMEM((heads * blocks, BLK, width), f32),
            pltpu.VMEM((BLK, near_width), f32),
            pltpu.VMEM((BLK, near_width), f32),
            pltpu.VMEM((BLK, near_width), f32),
            pltpu.VMEM((BLK, near_width), f32),
            pltpu.VMEM((4, BLK, width), f32),
            dma((inputs,)),
            dma((inputs,)),
            dma((inputs,)),
            dma((2,)),
            dma((8,)),
            dma((8,)),
            dma((len(NAMES),)),
            dma((len(NAMES),)),
            dma((len(NAMES) + 1,)),
            dma((len(NAMES) + 1,)),
            dma((2,)),
            dma((blocks,)),
            dma((2 * groups,)),
        ],
        compiler_params=pltpu.CompilerParams(
            collective_id=0, has_side_effects=True, vmem_limit_bytes=62 * 1024 * 1024
        ),
    )(slash, vertical, queries, kt, v)


def solution(mesh):
    in_specs = (
        P("seq", "head"),
        P("seq", "head"),
        P("seq", "head"),
        P("head", None),
        P("head", None),
    )
    out_specs = P(("seq", "head"), None)
    return jax.shard_map(shards, mesh=mesh, in_specs=in_specs, out_specs=out_specs, check_vma=False)
```

time: 170 us -> 102 us (0.60)
  the two profiles are of different devices: /device:TPU:103 before, /device:TPU:1 now
where the time goes in v1:
time: 102 us
  Pallas kernels  96.8 us (95%)
  local copies, waits for them, and re-layouts  4.92 us (5%)
    pallas_call x1, Pallas kernels, shards(): pl.pallas_call(functools.partial(layer_kernel, blocks=blocks, heads=heads...  96.8 us
    unnamed x1, local copies, waits for them, and re-layouts  3.13 us

profile of v1, /device:TPU:1, one launch (start us, length us, event | category | flops | bytes accessed | tf_op | source)
XLA Modules:
  0.0 101.8 jit_solution(4813652887272429472)
XLA Ops:
  0.0 1.8 %copy.6 = bf16[8,128,128]{1,2,0:T(8,128)(2,1)} copy(bf16[8,128,128]{2,1,0:T(8,128)(2,1)} %bitcast.5) | data formatting | bytes 524288 | tf_op jit(solution)/shard_map/reshape | solution.py:599
  1.8 96.8 %shard_map.55 = bf16[256,4096]{1,0:T(8,128)(2,1)} custom-call(s32[8,8]{1,0:T(8,128)} %slash_ref.1, s32[8,8]{1,0:T(8,128)} %vertical_ref.1, bf16[1024,1024]{1,0:T(8,128)(2,1)} %queries_ref.1, bf16[8,128,128]{2,1,0:T(8,128)(2,1)} %bitcast.3, bf16[8,128,128]{2,1,0:T(8,128)(2,1)} %bitcast.4), custom_call_target="tpu_custom_call" | custom-call | tf_op jit(solution)/shard_map/pallas_call | solution.py:606
  98.6 3.1 %copy.8 = bf16[256,4096]{1,0:T(8,128)(2,1)} copy(bf16[256,4096]{1,0:T(8,128)(2,1)} %shard_map.55) | data formatting | bytes 4194304

commit v2 on v1

--- a/solution.py
+++ b/solution.py
@@ -19,11 +19,11 @@
 MESH = pl.DeviceIdType.MESH
 
 COPIES = {}
-COPIES["zp"] = ((0, 1), (0, 0), "full")
 COPIES["zm"] = ((0, -1), (0, 0), "full")
 COPIES["xp"] = ((1, 0), (0, 0), "full")
 COPIES["xm"] = ((-1, 0), (0, 0), "full")
 COPIES["zm2"] = ((0, -1), (0, 1), "full")
+COPIES["zm3"] = ((0, -1), (0, 2), "full")
 COPIES["xm2"] = ((-1, 0), (1, 0), "full")
 for d in (1, -1, 2):
     COPIES["xpA", d] = ((1, 0), (0, d), "A")
@@ -37,39 +37,25 @@
 THEN = {name: [] for name in NAMES}
 THEN["zm"] = ["zm2", ("xpA", 1), ("xmA", 1)]
 THEN["zm2"] = [("xpA", 2), ("xmA", 2)]
-THEN["zp"] = [("xpA", -1), ("xmA", -1)]
-THEN["xm"] = ["xm2", ("zpB", 1), ("zmB", 1)]
-THEN["xm2"] = [("zpB", 2), ("zmB", 2)]
-THEN["xp"] = [("zpB", -1), ("zmB", -1)]
+THEN["zm3"] = [("xpA", -1), ("xmA", -1)]
+THEN["xm"] = ["xm2", ("zmB", 1)]
+THEN["xp"] = [("zmB", -1)]
+THEN["xm2"] = [("zmB", 2), ("zpB", 2)]
 for d in (1, -1, 2):
     THEN["xmA", d] = [("xmA2", d)]
     THEN["zmB", d] = [("zmB2", d)]
 
-FIRST = ["xm", "zm", "xp"]
-SECOND = ["xm2", "zm2", ("zmB", 1), ("xmA", 1), ("xpA", 1)]
+FIRST = ["zm", "xm", "xp"]
+SECOND = ["zm2", "xm2", ("zmB", 1), ("xmA", 1), ("xpA", 1), ("zmB", -1)]
 LATER = [
-    [("zmB", -1)],
-    [("xmA", 2)],
-    [("zmB", 2)],
-    ["zp"],
-    [("xpA", 2)],
-    [("zmB2", 1)],
-    [("xmA2", 1)],
-    [("zmB2", -1)],
-    [("xmA", -1)],
-    [("zpB", 1), ("xpA", -1)],
-    [("zmB2", 2), ("xmA2", 2)],
-    [("zpB", -1)],
-    [("zpB", 2), ("xmA2", -1)],
+    [("xmA", -1), ("xpA", -1)],
+    [("zpB", 1), ("zpB", -1)],
+    [("xmA", 2), ("zmB", 2)],
+    [("xpA", 2), ("zmB2", 1)],
+    [("xmA2", 1), ("zmB2", -1)],
+    [("xmA2", -1), ("zpB", 2)],
+    [("xmA2", 2), ("zmB2", 2)],
 ]
-
-
-def attended(slot, weights_of, blocks_of, pairs):
-    mixed = None
-    for n in range(pairs):
-        part = jnp.dot(weights_of(n), blocks_of(n), preferred_element_type=jnp.float32)
-        mixed = part if mixed is None else mixed + part
-    return mixed
 
 
 def layer_kernel(
@@ -85,6 +71,7 @@
     found_s,
     q_ref,
     own_ref,
+    hop_ref,
     near,
     far,
     staged,
@@ -139,8 +126,14 @@
     def worker_of(of_group):
         return {"seq": 2 * node + lax.rem(of_group, 2), "head": 2 * (of_group // 2) + low}
 
-    sources = [slash_ref, vertical_ref, kt_ref, v_ref]
-    targets = [table_v.at[0], table_v.at[1], own_ref.at[:, 0], own_ref.at[:, 1]]
+    sources = [slash_ref, vertical_ref]
+    targets = [table_v.at[0], table_v.at[1]]
+    for c in (1, 0):
+        for kv, ref in enumerate((kt_ref, v_ref)):
+            part = pl.ds(c * half, half)
+            sources.append(ref.at[part])
+            targets.append(own_ref.at[part, kv])
+    first_query = len(sources)
     for i in range(blocks):
         rows = pl.ds(i * BLK, BLK)
         sources.append(queries_ref.at[rows])
@@ -206,17 +199,19 @@
         return near.at[pl.ds((REACH - back) * blocks + c * half, half)]
 
     def hop_one(c):
-        return near_copy(own_ref.at[pl.ds(c * half, half)], near_part(2, c), c, follower)
+        part = pl.ds(c * half, half)
+        return near_copy(own_ref.at[part], hop_ref.at[part], c, follower)
 
     def hop_two(c):
-        return near_copy(near_part(2, c), near_part(4, c), 2 + c, follower)
+        return near_copy(hop_ref.at[pl.ds(c * half, half)], near_part(4, c), 2 + c, follower)
 
     def twin_one(c, from_own):
-        src = own_ref.at[pl.ds(c * half, half)] if from_own else near_part(2, c)
+        src = (own_ref if from_own else hop_ref).at[pl.ds(c * half, half)]
         return near_copy(src, near_part(1, c), 4 + c, twin)
 
-    def twin_two(c, back):
-        return near_copy(near_part(back, c), near_part(3, c), 6 + c, twin)
+    def twin_two(c, from_hop):
+        src = hop_ref.at[pl.ds(c * half, half)] if from_hop else near_part(4, c)
+        return near_copy(src, near_part(3, c), 6 + c, twin)
 
     def unit(dx, dz, part, of_core):
         to = lax.rem(x + dx + SIDE, SIDE) * SIDE + lax.rem(z + dz + SIDE, SIDE)
@@ -266,38 +261,25 @@
 
     def note_used(h, used):
         for n in range(listed):
-            block = table_s[1, h, n] - slab * blocks
-            used = tuple(u | (block == j).astype(jnp.int32) for j, u in enumerate(used))
+            block = table_s[1, h, n] - (slab - 2) * blocks
+            used = tuple(
+                u | (block == (j if j < blocks else j + blocks)).astype(jnp.int32)
+                for j, u in enumerate(used)
+            )
         return used
 
-    used = lax.fori_loop(0, heads, note_used, (jnp.int32(0),) * blocks)
-    picked = [jnp.int32(0)] * CAP
-    rank = jnp.int32(0)
-    for j in range(blocks):
-        picked = [jnp.where((used[j] == 1) & (rank == k), j, at_k) for k, at_k in enumerate(picked)]
-        rank = rank + used[j]
-
-    wait_input(2)
-    wait_input(3)
-    for c in (1, 0):
-        hop_one(c).start()
-
-    own_unit = pl.multiple_of((core * NODES + node) * CAP, CAP)
-    for k in range(CAP):
-        for kv in range(2):
-            far[own_unit + k, kv] = own_ref[picked[k], kv]
-
-    @pl.when(core == 0)
-    def _():
-        for c in range(2):
-            twin_one(c, True).start()
-
-    for name in ("xm", "zm", "xp"):
-        send(name).start()
-    share("own", core).start()
-    for j in range(blocks):
-        for kv in range(2):
-            near[REACH * blocks + j, kv] = own_ref[j, kv]
+    used = lax.fori_loop(0, heads, note_used, (jnp.int32(0),) * (2 * blocks))
+
+    def choose(used):
+        picked, rank = [jnp.int32(0)] * CAP, jnp.int32(0)
+        for j in range(blocks):
+            picked = [
+                jnp.where((used[j] == 1) & (rank == k), j, at_k) for k, at_k in enumerate(picked)
+            ]
+            rank = rank + used[j]
+        return picked
+
+    picked_before, picked = choose(used[:blocks]), choose(used[blocks:])
 
     verticals = table_v[1]
     first_of = verticals // blocks * blocks
@@ -315,6 +297,29 @@
     found_v[...] = ((of_slab % 2) * NODES + of_slab // 2) * CAP + place
     to_found = pltpu.make_async_copy(found_v, found_s, table_sem.at[1])
     to_found.start()
+
+    def pack(src, node_of, picked):
+        first = pl.multiple_of((core * NODES + node_of) * CAP, CAP)
+        for k in range(CAP):
+            for kv in range(2):
+                far[first + k, kv] = src[picked[k], kv]
+
+    for c in (1, 0):
+        for k in range(2):
+            wait_input(2 + 2 * (1 - c) + k)
+        hop_one(c).start()
+
+        @pl.when(core == 0)
+        def _():
+            twin_one(c, True).start()
+
+    pack(own_ref, node, picked)
+    for j in range(blocks):
+        for kv in range(2):
+            near[REACH * blocks + j, kv] = own_ref[j, kv]
+    for name in ("zm", "xm", "xp"):
+        send(name).start()
+    share("own", core).start()
     to_found.wait()
 
     for name in FIRST:
@@ -335,17 +340,37 @@
 
         @pl.when(core == 0)
         def _():
-            twin_two(c, 2).start()
-
-    send("zp").start()
+            twin_two(c, True).start()
+
+    @pl.when(z > 0)
+    def _():
+        pack(hop_ref, x * SIDE + z - 1, picked_before)
+
+    for j in range(blocks):
+        for kv in range(2):
+            near[2 * blocks + j, kv] = hop_ref[j, kv]
+
+    @pl.when(z > 0)
+    def _():
+        for following in THEN["zm3"]:
+            send(following).start()
+        share("zm3", core).start()
+
+    for d in (1, -1):
+        send(("zpB", d)).start()
     for name in SECOND:
         event(name)
+        if name == "zm2":
+
+            @pl.when(z == 1)
+            def _():
+                send("zm3").start()
 
     @pl.when(core == 1)
     def _():
         for c in (1, 0):
             hop_two(c).wait_recv()
-            twin_two(c, 4).start()
+            twin_two(c, False).start()
 
     @pl.when(core == 0)
     def _():
@@ -353,7 +378,11 @@
 
     for c in range(2):
         twin_one(c, True).wait_recv()
-        twin_two(c, 2).wait_recv()
+        twin_two(c, True).wait_recv()
+
+    @pl.when(z == 0)
+    def _():
+        event("zm3")
 
     factor = math.log2(math.e) / math.sqrt(width)
     causal = lax.broadcasted_iota(jnp.int32, (BLK, BLK), 0) >= lax.broadcasted_iota(
@@ -364,7 +393,8 @@
 
     def query(i, h):
         return q_ref[
-            pl.ds(pl.multiple_of(i * BLK, BLK), BLK), pl.ds(pl.multiple_of(h * width, width), width)
+            pl.ds(i * BLK if isinstance(i, int) else pl.multiple_of(i * BLK, BLK), BLK),
+            pl.ds(pl.multiple_of(h * width, width), width),
         ]
 
     def pair_scores(q, ref, a, b, bias_a, bias_b):
@@ -384,8 +414,8 @@
         offset = table_s[0, h, n]
         return REACH * blocks + i - offset, jnp.where(base + i >= offset, 0.0, NEG)
 
-    def near_scores(step, u):
-        i, h = step // heads, step % heads
+    def near_scores(i, h, u):
+        step = i * heads + h
         q = query(i, h)
         own = jnp.dot(q, near[REACH * blocks + i, 0], preferred_element_type=jnp.float32)
         own = jnp.where(causal, own, NEG)
@@ -502,30 +532,21 @@
         def _():
             out_copy(k).start()
 
-    def near_loop(k, carry):
-        for j, names in enumerate(LATER):
-
-            @pl.when(k == j + 1)
-            def _():
-                for name in names:
-                    event(name)
-
-        first = 4 * k
-        near_scores(first + 2, 2)
-        near_mix(first, 0)
-        near_scores(first + 3, 3)
-        near_mix(first + 1, 1)
-        near_scores(lax.rem(first + 4, steps), 0)
-        near_mix(first + 2, 2)
-        near_scores(lax.rem(first + 5, steps), 1)
-        near_mix(first + 3, 3)
+    def near_steps(i, k, carry):
+        first = i * heads + 4 * k
+        for u in range(4):
+            near_scores(i, 4 * k + u, u)
+            near_mix(lax.rem(first + steps + u - 2, steps), (u + 2) % 4)
         return carry
 
     for i in range(blocks):
-        wait_input(4 + i)
-    near_scores(0, 0)
-    near_scores(1, 1)
-    lax.fori_loop(0, steps // 4, near_loop, 0)
+        wait_input(first_query + i)
+        lax.fori_loop(0, heads // 4, functools.partial(near_steps, i), 0)
+        if i < len(LATER):
+            for name in LATER[i]:
+                event(name)
+    for u in (2, 3):
+        near_mix(steps - 4 + u, u)
 
     for name in NAMES:
         share(name, 1 - core).wait_recv()
@@ -560,7 +581,7 @@
     for c in range(2):
         hop_one(c).wait_send()
         twin_one(c, True).wait_send()
-        twin_two(c, 2).wait_send()
+        twin_two(c, True).wait_send()
     hop_two(1).wait_send()
 
     @pl.when(core == 1)
@@ -568,8 +589,14 @@
         hop_two(0).wait_send()
 
     for name in NAMES:
-        send(name).wait_send()
         share(name, core).wait_send()
+        if name != "zm3":
+            send(name).wait_send()
+
+    @pl.when(z == 1)
+    def _():
+        send("zm3").wait_send()
+
     share("own", core).wait_send()
 
     for k in range(blocks):
@@ -601,7 +628,7 @@
     dma = pltpu.SemaphoreType.DMA
     anywhere = pl.BlockSpec(memory_space=pl.ANY)
     bf16, f32 = jnp.bfloat16, jnp.float32
-    inputs = 4 + blocks
+    inputs = 6 + blocks
     near_width = (listed + 1) * BLK
     return pl.pallas_call(
         functools.partial(layer_kernel, blocks=blocks, heads=heads, width=width, listed=listed),
@@ -614,6 +641,7 @@
             pltpu.VMEM((heads, listed), jnp.int32),
             pltpu.SMEM((heads, listed), jnp.int32),
             pltpu.VMEM(queries.shape, bf16),
+            pltpu.VMEM((blocks, 2, BLK, width), bf16),
             pltpu.VMEM((blocks, 2, BLK, width), bf16),
             pltpu.VMEM(((REACH + 1) * blocks, 2, BLK, width), bf16),
             pltpu.VMEM((2 * NODES * CAP, 2, BLK, width), bf16),

time: 102 us -> 109 us (1.069)
  Pallas kernels: 96.8 us -> 104 us
    pallas_call x1, Pallas kernels: 96.8 us -> 104 us  [shards(): pl.pallas_call(functools.partial(layer_kernel, blocks=blocks, heads=heads...]
where the time goes in v2:
time: 109 us
  Pallas kernels  104 us (95%)
  local copies, waits for them, and re-layouts  4.92 us (5%)
    pallas_call x1, Pallas kernels, shards(): pl.pallas_call(functools.partial(layer_kernel, blocks=blocks, heads=heads...  104 us
    unnamed x1, local copies, waits for them, and re-layouts  3.13 us

profile of v2, /device:TPU:1, one launch (start us, length us, event | category | flops | bytes accessed | tf_op | source)
XLA Modules:
  0.0 108.6 jit_solution(1174165711186495840)
XLA Ops:
  0.0 1.8 %copy.6 = bf16[8,128,128]{1,2,0:T(8,128)(2,1)} copy(bf16[8,128,128]{2,1,0:T(8,128)(2,1)} %bitcast.5) | data formatting | bytes 524288 | tf_op jit(solution)/shard_map/reshape | solution.py:626
  1.8 103.7 %shard_map.55 = bf16[256,4096]{1,0:T(8,128)(2,1)} custom-call(s32[8,8]{1,0:T(8,128)} %slash_ref.1, s32[8,8]{1,0:T(8,128)} %vertical_ref.1, bf16[1024,1024]{1,0:T(8,128)(2,1)} %queries_ref.1, bf16[8,128,128]{2,1,0:T(8,128)(2,1)} %bitcast.3, bf16[8,128,128]{2,1,0:T(8,128)(2,1)} %bitcast.4), custom_call_target="tpu_custom_call" | custom-call | tf_op jit(solution)/shard_map/pallas_call | solution.py:633
  105.5 3.1 %copy.8 = bf16[256,4096]{1,0:T(8,128)(2,1)} copy(bf16[256,4096]{1,0:T(8,128)(2,1)} %shard_map.55) | data formatting | bytes 4194304

commit v3 on v2

--- a/solution.py
+++ b/solution.py
@@ -39,22 +39,20 @@
 THEN["zm2"] = [("xpA", 2), ("xmA", 2)]
 THEN["zm3"] = [("xpA", -1), ("xmA", -1)]
 THEN["xm"] = ["xm2", ("zmB", 1)]
-THEN["xp"] = [("zmB", -1)]
+THEN["xp"] = [("zmB", -1), ("zpB", -1)]
 THEN["xm2"] = [("zmB", 2), ("zpB", 2)]
 for d in (1, -1, 2):
     THEN["xmA", d] = [("xmA2", d)]
     THEN["zmB", d] = [("zmB2", d)]
 
-FIRST = ["zm", "xm", "xp"]
-SECOND = ["zm2", "xm2", ("zmB", 1), ("xmA", 1), ("xpA", 1), ("zmB", -1)]
+FIRST = ["zm", "xm"]
+SECOND = ["zm2", "xm2", ("zmB", 1), ("xmA", 1)]
+THIRD = [("xmA", 2), ("zmB", 2)]
 LATER = [
-    [("xmA", -1), ("xpA", -1)],
-    [("zpB", 1), ("zpB", -1)],
-    [("xmA", 2), ("zmB", 2)],
-    [("xpA", 2), ("zmB2", 1)],
-    [("xmA2", 1), ("zmB2", -1)],
-    [("xmA2", -1), ("zpB", 2)],
+    [("xmA", -1), ("zmB", -1), ("zmB2", 1), ("xmA2", 1)],
     [("xmA2", 2), ("zmB2", 2)],
+    [("xmA2", -1), ("zmB2", -1)],
+    [(name, d) for d in (1, -1, 2) for name in ("xpA", "zpB")],
 ]
 
 
@@ -69,6 +67,7 @@
     table_s,
     found_v,
     found_s,
+    picked_s,
     q_ref,
     own_ref,
     hop_ref,
@@ -82,6 +81,10 @@
     scores_1,
     scores_2,
     scores_3,
+    weights_0,
+    weights_1,
+    weights_2,
+    weights_3,
     tops,
     load_sem,
     swap_send,
@@ -109,6 +112,7 @@
     group, slab = 2 * high + low, 2 * node + core
     native = low == core
     scores = (scores_0, scores_1, scores_2, scores_3)
+    weights = (weights_0, weights_1, weights_2, weights_3)
     half = blocks // 2
 
     def at(dx, dz):
@@ -125,6 +129,11 @@
 
     def worker_of(of_group):
         return {"seq": 2 * node + lax.rem(of_group, 2), "head": 2 * (of_group // 2) + low}
+
+    def row_block(k):
+        late = k // half
+        quarter = 2 * ((1 - late) * (1 - high) + late * high) + (k % half) // 2
+        return 2 * quarter + k % 2
 
     sources = [slash_ref, vertical_ref]
     targets = [table_v.at[0], table_v.at[1]]
@@ -134,8 +143,8 @@
             sources.append(ref.at[part])
             targets.append(own_ref.at[part, kv])
     first_query = len(sources)
-    for i in range(blocks):
-        rows = pl.ds(i * BLK, BLK)
+    for k in range(blocks):
+        rows = pl.ds(pl.multiple_of(row_block(k) * BLK, BLK), BLK)
         sources.append(queries_ref.at[rows])
         targets.append(q_ref.at[rows])
 
@@ -157,6 +166,55 @@
         def _():
             swap(k).wait_recv()
 
+    def prepare(wait_table):
+        for k in range(2):
+            wait_table(k)
+        to_scalars = pltpu.make_async_copy(table_v, table_s, table_sem.at[0])
+        to_scalars.start()
+        to_scalars.wait()
+
+        def note_used(h, used):
+            for n in range(listed):
+                block = table_s[1, h, n] - (slab - 2) * blocks
+                used = tuple(
+                    u | (block == (j if j < blocks else j + blocks)).astype(jnp.int32)
+                    for j, u in enumerate(used)
+                )
+            return used
+
+        used = lax.fori_loop(0, heads, note_used, (jnp.int32(0),) * (2 * blocks))
+
+        def choose(used):
+            picked, rank = [jnp.int32(0)] * CAP, jnp.int32(0)
+            for j in range(blocks):
+                picked = [
+                    jnp.where((used[j] == 1) & (rank == k), j, at_k) for k, at_k in enumerate(picked)
+                ]
+                rank = rank + used[j]
+            return picked
+
+        for c in range(2):
+            for k, block in enumerate(choose(used[c * blocks : (c + 1) * blocks])):
+                picked_s[c, k] = block
+
+        verticals = table_v[1]
+        first_of = verticals // blocks * blocks
+        seen = jnp.zeros_like(verticals)
+        for h in range(heads):
+            for n in range(listed):
+                there = table_s[1, h, n] - first_of
+                for j in range(blocks - 1):
+                    seen = seen | jnp.where(there == j, 1 << j, 0)
+        before = verticals - first_of
+        place = jnp.zeros_like(verticals)
+        for j in range(blocks - 1):
+            place = place + jnp.where((before > j) & (seen & (1 << j) != 0), 1, 0)
+        of_slab = verticals // blocks
+        found_v[...] = ((of_slab % 2) * NODES + of_slab // 2) * CAP + place
+        to_found = pltpu.make_async_copy(found_v, found_s, table_sem.at[1])
+        to_found.start()
+        to_found.wait()
+
     @pl.when(native)
     def _():
         for k in range(len(sources)):
@@ -183,12 +241,17 @@
     def _():
         greet(counterpart)
 
+    @pl.when(native)
+    def _():
+        prepare(lambda k: load(k).wait())
+
     pl.semaphore_wait(barrier, 7 + 6 + 3 * (low - core) * (low - core))
 
     @pl.when(jnp.logical_not(native))
     def _():
         for k in range(len(sources)):
             swap(k).start()
+        prepare(lambda k: swap(k).wait_recv())
 
     def near_copy(src, dst, k, device):
         return pltpu.make_async_remote_copy(
@@ -247,62 +310,29 @@
             ref, ref, twin_send.at[k], twin_recv.at[k], device_id=twin, device_id_type=MESH
         )
 
+    def start(name):
+        if name[0] == "zpB":
+            return
+        if name == "xp" or name[0] == "xpA":
+
+            @pl.when(z < SIDE - 1)
+            def _():
+                send(name).start()
+
+        else:
+            send(name).start()
+
     def event(name):
         receive(name).wait_recv()
         for following in THEN[name]:
-            send(following).start()
+            start(following)
         share(name, core).start()
 
-    wait_input(0)
-    wait_input(1)
-    to_scalars = pltpu.make_async_copy(table_v, table_s, table_sem.at[0])
-    to_scalars.start()
-    to_scalars.wait()
-
-    def note_used(h, used):
-        for n in range(listed):
-            block = table_s[1, h, n] - (slab - 2) * blocks
-            used = tuple(
-                u | (block == (j if j < blocks else j + blocks)).astype(jnp.int32)
-                for j, u in enumerate(used)
-            )
-        return used
-
-    used = lax.fori_loop(0, heads, note_used, (jnp.int32(0),) * (2 * blocks))
-
-    def choose(used):
-        picked, rank = [jnp.int32(0)] * CAP, jnp.int32(0)
-        for j in range(blocks):
-            picked = [
-                jnp.where((used[j] == 1) & (rank == k), j, at_k) for k, at_k in enumerate(picked)
-            ]
-            rank = rank + used[j]
-        return picked
-
-    picked_before, picked = choose(used[:blocks]), choose(used[blocks:])
-
-    verticals = table_v[1]
-    first_of = verticals // blocks * blocks
-    seen = jnp.zeros_like(verticals)
-    for h in range(heads):
-        for n in range(listed):
-            there = table_s[1, h, n] - first_of
-            for j in range(blocks - 1):
-                seen = seen | jnp.where(there == j, 1 << j, 0)
-    before = verticals - first_of
-    place = jnp.zeros_like(verticals)
-    for j in range(blocks - 1):
-        place = place + jnp.where((before > j) & (seen & (1 << j) != 0), 1, 0)
-    of_slab = verticals // blocks
-    found_v[...] = ((of_slab % 2) * NODES + of_slab // 2) * CAP + place
-    to_found = pltpu.make_async_copy(found_v, found_s, table_sem.at[1])
-    to_found.start()
-
-    def pack(src, node_of, picked):
+    def pack(src, node_of, c):
         first = pl.multiple_of((core * NODES + node_of) * CAP, CAP)
         for k in range(CAP):
             for kv in range(2):
-                far[first + k, kv] = src[picked[k], kv]
+                far[first + k, kv] = src[picked_s[c, k], kv]
 
     for c in (1, 0):
         for k in range(2):
@@ -313,14 +343,13 @@
         def _():
             twin_one(c, True).start()
 
-    pack(own_ref, node, picked)
+    pack(own_ref, node, 1)
     for j in range(blocks):
         for kv in range(2):
             near[REACH * blocks + j, kv] = own_ref[j, kv]
     for name in ("zm", "xm", "xp"):
-        send(name).start()
+        start(name)
     share("own", core).start()
-    to_found.wait()
 
     for name in FIRST:
         event(name)
@@ -344,7 +373,7 @@
 
     @pl.when(z > 0)
     def _():
-        pack(hop_ref, x * SIDE + z - 1, picked_before)
+        pack(hop_ref, x * SIDE + z - 1, 0)
 
     for j in range(blocks):
         for kv in range(2):
@@ -353,11 +382,17 @@
     @pl.when(z > 0)
     def _():
         for following in THEN["zm3"]:
-            send(following).start()
+            start(following)
         share("zm3", core).start()
 
-    for d in (1, -1):
-        send(("zpB", d)).start()
+    @pl.when(z == SIDE - 1)
+    def _():
+        send("xp").start()
+
+    @pl.when(z < SIDE - 1)
+    def _():
+        event("xp")
+
     for name in SECOND:
         event(name)
         if name == "zm2":
@@ -366,6 +401,17 @@
             def _():
                 send("zm3").start()
 
+    @pl.when(z == SIDE - 1)
+    def _():
+        event("xp")
+
+    @pl.when(z == 0)
+    def _():
+        event("zm3")
+
+    for name in THIRD:
+        event(name)
+
     @pl.when(core == 1)
     def _():
         for c in (1, 0):
@@ -380,9 +426,13 @@
         twin_one(c, True).wait_recv()
         twin_two(c, True).wait_recv()
 
-    @pl.when(z == 0)
-    def _():
-        event("zm3")
+    for d in (1, -1, 2):
+        send(("zpB", d)).start()
+
+    @pl.when(z == SIDE - 1)
+    def _():
+        for d in (1, -1, 2):
+            send(("xpA", d)).start()
 
     factor = math.log2(math.e) / math.sqrt(width)
     causal = lax.broadcasted_iota(jnp.int32, (BLK, BLK), 0) >= lax.broadcasted_iota(
@@ -393,7 +443,7 @@
 
     def query(i, h):
         return q_ref[
-            pl.ds(i * BLK if isinstance(i, int) else pl.multiple_of(i * BLK, BLK), BLK),
+            pl.ds(pl.multiple_of(i * BLK, BLK), BLK),
             pl.ds(pl.multiple_of(h * width, width), width),
         ]
 
@@ -403,56 +453,55 @@
         )
         return pair[:, :BLK] + bias_a, pair[:, BLK:] + bias_b
 
-    def pair_mix(ref, a, b, wa, wb):
+    def pair_mix(u, n, ref, a, b):
         return jnp.dot(
-            jnp.concatenate([wa.astype(jnp.bfloat16), wb.astype(jnp.bfloat16)], axis=1),
+            weights[u][:, n * BLK : (n + 2) * BLK],
             jnp.concatenate([ref[a, 1], ref[b, 1]], axis=0),
             preferred_element_type=jnp.float32,
         )
+
+    def row_top(u, count):
+        top = scores[u][:, :BLK]
+        for n in range(1, count):
+            top = jnp.maximum(top, scores[u][:, n * BLK : (n + 1) * BLK])
+        return jnp.broadcast_to(jnp.max(top, axis=1, keepdims=True) * factor, (BLK, width))
+
+    def weigh(u, count, top):
+        total = None
+        for n in range(count):
+            w = jnp.exp2(scores[u][:, n * BLK : (n + 1) * BLK] * factor - top)
+            total = w if total is None else total + w
+            weights[u][:, n * BLK : (n + 1) * BLK] = w.astype(jnp.bfloat16)
+        return jnp.broadcast_to(jnp.sum(total, axis=1, keepdims=True), (BLK, width))
 
     def near_entry(i, h, n):
         offset = table_s[0, h, n]
         return REACH * blocks + i - offset, jnp.where(base + i >= offset, 0.0, NEG)
 
-    def near_scores(i, h, u):
-        step = i * heads + h
+    def near_scores(k, h, u):
+        i = row_block(k)
         q = query(i, h)
         own = jnp.dot(q, near[REACH * blocks + i, 0], preferred_element_type=jnp.float32)
-        own = jnp.where(causal, own, NEG)
-        scores[u][:, :BLK] = own
-        top = own
+        scores[u][:, :BLK] = jnp.where(causal, own, NEG)
         for n in range(0, listed, 2):
             (a, bias_a), (b, bias_b) = near_entry(i, h, n), near_entry(i, h, n + 1)
             sa, sb = pair_scores(q, near, a, b, bias_a, bias_b)
             scores[u][:, (n + 1) * BLK : (n + 2) * BLK] = sa
             scores[u][:, (n + 2) * BLK : (n + 3) * BLK] = sb
-            top = jnp.maximum(top, jnp.maximum(sa, sb))
-        top = jnp.max(top, axis=1, keepdims=True) * factor
-        top_ref[step] = jnp.broadcast_to(top, (BLK, width))
+
+    def near_weigh(step, u):
+        top_ref[step] = row_top(u, listed + 1)
+        total_ref[step] = weigh(u, listed + 1, top_ref[step])
 
     def near_mix(step, u):
-        i, h = step // heads, step % heads
-        top = top_ref[step]
-
-        def weight(n):
-            return jnp.exp2(scores[u][:, n * BLK : (n + 1) * BLK] * factor - top)
-
-        total = weight(0)
+        i, h = row_block(step // heads), step % heads
         mixed = jnp.dot(
-            total.astype(jnp.bfloat16), near[REACH * blocks + i, 1], preferred_element_type=jnp.float32
+            weights[u][:, :BLK], near[REACH * blocks + i, 1], preferred_element_type=jnp.float32
         )
         for n in range(0, listed, 2):
             a, b = near_entry(i, h, n)[0], near_entry(i, h, n + 1)[0]
-            wa, wb = weight(n + 1), weight(n + 2)
-            total = total + (wa + wb)
-            mixed = mixed + pair_mix(near, a, b, wa, wb)
+            mixed = mixed + pair_mix(u, n + 1, near, a, b)
         mixed_ref[step] = mixed
-        total_ref[step] = jnp.broadcast_to(jnp.sum(total, axis=1, keepdims=True), (BLK, width))
-
-    def row_block(k):
-        late = k // half
-        quarter = 2 * ((1 - late) * (1 - high) + late * high) + (k % half) // 2
-        return 2 * quarter + k % 2
 
     def far_bias(own, h, block):
         gap = own - block
@@ -473,21 +522,25 @@
             both = jnp.maximum(sa, sb)
             top = both if top is None else jnp.maximum(top, both)
         top = jnp.max(top, axis=1, keepdims=True) * factor
-        tops[u] = jnp.maximum(jnp.broadcast_to(top, (BLK, width)), top_ref[i * heads + h])
+        tops[u] = jnp.maximum(jnp.broadcast_to(top, (BLK, width)), top_ref[step])
 
     def far_mix(step, u):
         i, h = row_block(step // heads), step % heads
-        top, kept = tops[u], i * heads + h
-        scale = jnp.exp2(top_ref[kept] - top)
+        top = tops[u]
+        scale = jnp.exp2(top_ref[step] - top)
         total, mixed = None, None
         for n in range(0, listed, 2):
             wa = jnp.exp2(scores[u][:, n * BLK : (n + 1) * BLK] * factor - top)
             wb = jnp.exp2(scores[u][:, (n + 1) * BLK : (n + 2) * BLK] * factor - top)
             total = wa + wb if total is None else total + (wa + wb)
-            part = pair_mix(far, found_s[h, n], found_s[h, n + 1], wa, wb)
+            part = jnp.dot(
+                jnp.concatenate([wa.astype(jnp.bfloat16), wb.astype(jnp.bfloat16)], axis=1),
+                jnp.concatenate([far[found_s[h, n], 1], far[found_s[h, n + 1], 1]], axis=0),
+                preferred_element_type=jnp.float32,
+            )
             mixed = part if mixed is None else mixed + part
-        total = jnp.sum(total, axis=1, keepdims=True) + total_ref[kept] * scale
-        mixed = mixed + mixed_ref[kept] * scale
+        total = jnp.sum(total, axis=1, keepdims=True) + total_ref[step] * scale
+        mixed = mixed + mixed_ref[step] * scale
         rows = pl.ds(pl.multiple_of(i * BLK, BLK), BLK)
         staged[rows, pl.ds(pl.multiple_of(h * width, width), width)] = (mixed / total).astype(jnp.bfloat16)
 
@@ -532,46 +585,52 @@
         def _():
             out_copy(k).start()
 
-    def near_steps(i, k, carry):
-        first = i * heads + 4 * k
+    def near_steps(k, j, carry):
+        first = k * heads + 4 * j
         for u in range(4):
-            near_scores(i, 4 * k + u, u)
+            near_scores(k, 4 * j + u, u)
+            near_weigh(lax.rem(first + steps + u - 1, steps), (u + 3) % 4)
             near_mix(lax.rem(first + steps + u - 2, steps), (u + 2) % 4)
         return carry
 
-    for i in range(blocks):
-        wait_input(first_query + i)
-        lax.fori_loop(0, heads // 4, functools.partial(near_steps, i), 0)
-        if i < len(LATER):
-            for name in LATER[i]:
+    def near_group(ks):
+        for k in ks:
+            lax.fori_loop(0, heads // 4, functools.partial(near_steps, k), 0)
+            for name in LATER[k] if k < len(LATER) else []:
                 event(name)
-    for u in (2, 3):
-        near_mix(steps - 4 + u, u)
-
+        last = (ks[-1] + 1) * heads
+        near_weigh(jnp.int32(last - 1), 3)
+        for u in (2, 3):
+            near_mix(jnp.int32(last - 4 + u), u)
+
+    def far_group(ks):
+        count, before = len(ks) * heads, ks[0] * heads
+
+        def far_steps(j, carry):
+            first = 4 * j
+            for u in range(4):
+                far_scores(before + lax.rem(first + u + 2, count), (u + 2) % 4)
+                far_mix(before + first + u, u)
+
+            @pl.when(j % 2 == 1)
+            def _():
+                send_block(ks[0] + j // 2)
+
+            return carry
+
+        for u in range(2):
+            far_scores(jnp.int32(before + u), u)
+        lax.fori_loop(0, count // 4, far_steps, 0)
+
+    for k in range(blocks):
+        wait_input(first_query + k)
+    near_group(range(half))
     for name in NAMES:
         share(name, 1 - core).wait_recv()
     share("own", 1 - core).wait_recv()
-
-    def far_loop(k, carry):
-        first = 4 * k
-        far_scores(first + 2, 2)
-        far_mix(first, 0)
-        far_scores(first + 3, 3)
-        far_mix(first + 1, 1)
-        far_scores(lax.rem(first + 4, steps), 0)
-        far_mix(first + 2, 2)
-        far_scores(lax.rem(first + 5, steps), 1)
-        far_mix(first + 3, 3)
-
-        @pl.when(k % 2 == 1)
-        def _():
-            send_block(k // 2)
-
-        return carry
-
-    far_scores(0, 0)
-    far_scores(1, 1)
-    lax.fori_loop(0, steps // 4, far_loop, 0)
+    far_group(range(half))
+    near_group(range(half, blocks))
+    far_group(range(half, blocks))
 
     @pl.when(jnp.logical_not(native))
     def _():
@@ -640,6 +699,7 @@
             pltpu.SMEM((2, heads, listed), jnp.int32),
             pltpu.VMEM((heads, listed), jnp.int32),
             pltpu.SMEM((heads, listed), jnp.int32),
+            pltpu.SMEM((2, CAP), jnp.int32),
             pltpu.VMEM(queries.shape, bf16),
             pltpu.VMEM((blocks, 2, BLK, width), bf16),
             pltpu.VMEM((blocks, 2, BLK, width), bf16),
@@ -653,6 +713,10 @@
             pltpu.VMEM((BLK, near_width), f32),
             pltpu.VMEM((BLK, near_width), f32),
             pltpu.VMEM((BLK, near_width), f32),
+            pltpu.VMEM((BLK, near_width), bf16),
+            pltpu.VMEM((BLK, near_width), bf16),
+            pltpu.VMEM((BLK, near_width), bf16),
+            pltpu.VMEM((BLK, near_width), bf16),
             pltpu.VMEM((4, BLK, width), f32),
             dma((inputs,)),
             dma((inputs,)),

time: 109 us -> 93.5 us (0.86)
  Pallas kernels: 104 us -> 88.2 us
    pallas_call x1, Pallas kernels: 104 us -> 88.2 us  [shards(): pl.pallas_call(functools.partial(layer_kernel, blocks=blocks, heads=heads...]
where the time goes in v3:
time: 93.5 us; the launch traced here: 93.1 us
  Pallas kernels  88.2 us (94%)
  local copies, waits for them, and re-layouts  4.92 us (5%)
    pallas_call x1, Pallas kernels, shards(): pl.pallas_call(functools.partial(layer_kernel, blocks=blocks, heads=heads...  88.2 us
    unnamed x1, local copies, waits for them, and re-layouts  3.13 us

profile of v3, /device:TPU:1, one launch (start us, length us, event | category | flops | bytes accessed | tf_op | source)
XLA Modules:
  0.0 93.1 jit_solution(9947755871156057501)
XLA Ops:
  0.0 1.8 %copy.6 = bf16[8,128,128]{1,2,0:T(8,128)(2,1)} copy(bf16[8,128,128]{2,1,0:T(8,128)(2,1)} %bitcast.5) | data formatting | bytes 524288 | tf_op jit(solution)/shard_map/reshape | solution.py:685
  1.8 88.2 %shard_map.55 = bf16[256,4096]{1,0:T(8,128)(2,1)} custom-call(s32[8,8]{1,0:T(8,128)} %slash_ref.1, s32[8,8]{1,0:T(8,128)} %vertical_ref.1, bf16[1024,1024]{1,0:T(8,128)(2,1)} %queries_ref.1, bf16[8,128,128]{2,1,0:T(8,128)(2,1)} %bitcast.3, bf16[8,128,128]{2,1,0:T(8,128)(2,1)} %bitcast.4), custom_call_target="tpu_custom_call" | custom-call | tf_op jit(solution)/shard_map/pallas_call | solution.py:692
  90.0 3.1 %copy.8 = bf16[256,4096]{1,0:T(8,128)(2,1)} copy(bf16[256,4096]{1,0:T(8,128)(2,1)} %shard_map.55) | data formatting | bytes 4194304

commit v4 on v3

--- a/solution.py
+++ b/solution.py
@@ -23,7 +23,7 @@
 COPIES["xp"] = ((1, 0), (0, 0), "full")
 COPIES["xm"] = ((-1, 0), (0, 0), "full")
 COPIES["zm2"] = ((0, -1), (0, 1), "full")
-COPIES["zm3"] = ((0, -1), (0, 2), "full")
+COPIES["zp"] = ((0, 1), (0, 0), "full")
 COPIES["xm2"] = ((-1, 0), (1, 0), "full")
 for d in (1, -1, 2):
     COPIES["xpA", d] = ((1, 0), (0, d), "A")
@@ -37,7 +37,7 @@
 THEN = {name: [] for name in NAMES}
 THEN["zm"] = ["zm2", ("xpA", 1), ("xmA", 1)]
 THEN["zm2"] = [("xpA", 2), ("xmA", 2)]
-THEN["zm3"] = [("xpA", -1), ("xmA", -1)]
+THEN["zp"] = [("xpA", -1), ("xmA", -1)]
 THEN["xm"] = ["xm2", ("zmB", 1)]
 THEN["xp"] = [("zmB", -1), ("zpB", -1)]
 THEN["xm2"] = [("zmB", 2), ("zpB", 2)]
@@ -47,10 +47,9 @@
 
 FIRST = ["zm", "xm"]
 SECOND = ["zm2", "xm2", ("zmB", 1), ("xmA", 1)]
-THIRD = [("xmA", 2), ("zmB", 2)]
 LATER = [
-    [("xmA", -1), ("zmB", -1), ("zmB2", 1), ("xmA2", 1)],
-    [("xmA2", 2), ("zmB2", 2)],
+    ["xp", "zp", ("xmA", 2), ("zmB", 2), ("zmB2", 1), ("xmA2", 1)],
+    [("zmB", -1), ("xmA", -1), ("xmA2", 2), ("zmB2", 2)],
     [("xmA2", -1), ("zmB2", -1)],
     [(name, d) for d in (1, -1, 2) for name in ("xpA", "zpB")],
 ]
@@ -68,7 +67,8 @@
     found_v,
     found_s,
     picked_s,
-    q_ref,
+    early_q,
+    late_q,
     own_ref,
     hop_ref,
     near,
@@ -146,7 +146,7 @@
     for k in range(blocks):
         rows = pl.ds(pl.multiple_of(row_block(k) * BLK, BLK), BLK)
         sources.append(queries_ref.at[rows])
-        targets.append(q_ref.at[rows])
+        targets.append((early_q if k < half else late_q).at[pl.ds(k % half * BLK, BLK)])
 
     def load(k):
         return pltpu.make_async_copy(sources[k], targets[k], load_sem.at[k])
@@ -381,12 +381,13 @@
 
     @pl.when(z > 0)
     def _():
-        for following in THEN["zm3"]:
+        for following in THEN["zp"]:
             start(following)
-        share("zm3", core).start()
+        share("zp", core).start()
 
     @pl.when(z == SIDE - 1)
     def _():
+        send("zp").start()
         send("xp").start()
 
     @pl.when(z < SIDE - 1)
@@ -394,22 +395,6 @@
         event("xp")
 
     for name in SECOND:
-        event(name)
-        if name == "zm2":
-
-            @pl.when(z == 1)
-            def _():
-                send("zm3").start()
-
-    @pl.when(z == SIDE - 1)
-    def _():
-        event("xp")
-
-    @pl.when(z == 0)
-    def _():
-        event("zm3")
-
-    for name in THIRD:
         event(name)
 
     @pl.when(core == 1)
@@ -426,8 +411,12 @@
         twin_one(c, True).wait_recv()
         twin_two(c, True).wait_recv()
 
-    for d in (1, -1, 2):
+    for d in (1, 2):
         send(("zpB", d)).start()
+
+    @pl.when(z < SIDE - 1)
+    def _():
+        send(("zpB", -1)).start()
 
     @pl.when(z == SIDE - 1)
     def _():
@@ -438,12 +427,12 @@
     causal = lax.broadcasted_iota(jnp.int32, (BLK, BLK), 0) >= lax.broadcasted_iota(
         jnp.int32, (BLK, BLK), 1
     )
-    steps = heads * blocks
+    kept = heads * half
     base = slab * blocks
 
-    def query(i, h):
-        return q_ref[
-            pl.ds(pl.multiple_of(i * BLK, BLK), BLK),
+    def query(ref, k, h):
+        return ref[
+            pl.ds(pl.multiple_of(k % half * BLK, BLK), BLK),
             pl.ds(pl.multiple_of(h * width, width), width),
         ]
 
@@ -480,7 +469,7 @@
 
     def near_scores(k, h, u):
         i = row_block(k)
-        q = query(i, h)
+        q = query(early_q, k, h)
         own = jnp.dot(q, near[REACH * blocks + i, 0], preferred_element_type=jnp.float32)
         scores[u][:, :BLK] = jnp.where(causal, own, NEG)
         for n in range(0, listed, 2):
@@ -512,7 +501,7 @@
 
     def far_scores(step, u):
         i, h = row_block(step // heads), step % heads
-        q = query(i, h)
+        q = query(early_q, step // heads, h)
         top = None
         for n in range(0, listed, 2):
             bias = [far_bias(base + i, h, table_s[1, h, n + d]) for d in range(2)]
@@ -544,60 +533,74 @@
         rows = pl.ds(pl.multiple_of(i * BLK, BLK), BLK)
         staged[rows, pl.ds(pl.multiple_of(h * width, width), width)] = (mixed / total).astype(jnp.bfloat16)
 
-    columns = pl.ds(pl.multiple_of(group * heads * width, heads * width), heads * width)
-
-    def out_copy(k):
+    part = heads * width // 2
+
+    def out_refs(k, c):
         i = row_block(k)
-        owner, n = i // 2, k % 2
+        here = staged.at[
+            pl.ds(pl.multiple_of(i * BLK, BLK), BLK), pl.ds(pl.multiple_of(c * part, part), part)
+        ]
+        first = pl.multiple_of((group * 2 + c) * part, part)
+        return here, out_ref.at[pl.ds(pl.multiple_of(k % 2 * BLK, BLK), BLK), pl.ds(first, part)]
+
+    def out_copy(k, c):
+        here, there = out_refs(k, c)
         return pltpu.make_async_remote_copy(
-            staged.at[pl.ds(pl.multiple_of(i * BLK, BLK), BLK)],
-            out_ref.at[pl.ds(pl.multiple_of(n * BLK, BLK), BLK), columns],
-            out_send.at[k], out_recv.at[group * 2 + n],
-            device_id=owner_of(owner), device_id_type=MESH,
-        )
-
-    def out_keep(k):
-        i = row_block(k)
-        n = k % 2
-        return pltpu.make_async_copy(
-            staged.at[pl.ds(pl.multiple_of(i * BLK, BLK), BLK)],
-            out_ref.at[pl.ds(pl.multiple_of(n * BLK, BLK), BLK), columns],
-            out_local.at[n],
-        )
+            here, there, out_send.at[k * 2 + c], out_recv.at[group * 4 + k % 2 * 2 + c],
+            device_id=owner_of(row_block(k) // 2), device_id_type=MESH,
+        )
+
+    def out_keep(k, c):
+        here, there = out_refs(k, c)
+        return pltpu.make_async_copy(here, there, out_local.at[k % 2 * 2 + c])
 
     def kept_here(k):
         return native & (row_block(k) // 2 == head)
 
-    def out_in(of_group, n):
+    def out_in(of_group, n, c):
         return pltpu.make_async_remote_copy(
-            staged.at[pl.ds(0, BLK)],
-            out_ref.at[pl.ds(n * BLK, BLK), pl.ds(of_group * heads * width, heads * width)],
-            out_send.at[0], out_recv.at[of_group * 2 + n],
+            staged.at[pl.ds(0, BLK), pl.ds(0, part)],
+            out_ref.at[pl.ds(n * BLK, BLK), pl.ds((of_group * 2 + c) * part, part)],
+            out_send.at[0], out_recv.at[of_group * 4 + n * 2 + c],
             device_id=worker_of(jnp.int32(of_group)), device_id_type=MESH,
         )
 
-    def send_block(k):
+    def send_part(k, c):
         @pl.when(kept_here(k))
         def _():
-            out_keep(k).start()
+            out_keep(k, c).start()
 
         @pl.when(jnp.logical_not(kept_here(k)))
         def _():
-            out_copy(k).start()
+            out_copy(k, c).start()
 
     def near_steps(k, j, carry):
         first = k * heads + 4 * j
         for u in range(4):
             near_scores(k, 4 * j + u, u)
-            near_weigh(lax.rem(first + steps + u - 1, steps), (u + 3) % 4)
-            near_mix(lax.rem(first + steps + u - 2, steps), (u + 2) % 4)
+            near_weigh(lax.rem(first + kept + u - 1, kept), (u + 3) % 4)
+            near_mix(lax.rem(first + kept + u - 2, kept), (u + 2) % 4)
         return carry
 
     def near_group(ks):
         for k in ks:
             lax.fori_loop(0, heads // 4, functools.partial(near_steps, k), 0)
             for name in LATER[k] if k < len(LATER) else []:
-                event(name)
+                if name == "xp":
+
+                    @pl.when(z == SIDE - 1)
+                    def _():
+                        event("xp")
+                        send(("zpB", -1)).start()
+
+                elif name == "zp":
+
+                    @pl.when(z == 0)
+                    def _():
+                        event("zp")
+
+                else:
+                    event(name)
         last = (ks[-1] + 1) * heads
         near_weigh(jnp.int32(last - 1), 3)
         for u in (2, 3):
@@ -612,25 +615,87 @@
                 far_scores(before + lax.rem(first + u + 2, count), (u + 2) % 4)
                 far_mix(before + first + u, u)
 
-            @pl.when(j % 2 == 1)
-            def _():
-                send_block(ks[0] + j // 2)
-
+            send_part(ks[0] + j // 2, j % 2)
             return carry
 
         for u in range(2):
             far_scores(jnp.int32(before + u), u)
         lax.fori_loop(0, count // 4, far_steps, 0)
 
-    for k in range(blocks):
+    def full_scores(step, u):
+        k, h = step // heads, step % heads
+        i = row_block(k)
+        q = query(late_q, k, h)
+        own = jnp.dot(q, near[REACH * blocks + i, 0], preferred_element_type=jnp.float32)
+        own = jnp.where(causal, own, NEG)
+        scores[u][:, :BLK] = own
+        top = own
+        for n in range(0, 2 * listed, 2):
+            if n < listed:
+                ref = near
+                (a, bias_a), (b, bias_b) = near_entry(i, h, n), near_entry(i, h, n + 1)
+            else:
+                ref, m = far, n - listed
+                a, b = found_s[h, m], found_s[h, m + 1]
+                bias_a, bias_b = (far_bias(base + i, h, table_s[1, h, m + d]) for d in range(2))
+            sa, sb = pair_scores(q, ref, a, b, bias_a, bias_b)
+            scores[u][:, (n + 1) * BLK : (n + 2) * BLK] = sa
+            scores[u][:, (n + 2) * BLK : (n + 3) * BLK] = sb
+            top = jnp.maximum(top, jnp.maximum(sa, sb))
+        tops[u] = jnp.broadcast_to(jnp.max(top, axis=1, keepdims=True) * factor, (BLK, width))
+
+    def full_mix(step, u):
+        i, h = row_block(step // heads), step % heads
+        top = tops[u]
+
+        def weight(n):
+            return jnp.exp2(scores[u][:, n * BLK : (n + 1) * BLK] * factor - top)
+
+        total = weight(0)
+        mixed = jnp.dot(
+            total.astype(jnp.bfloat16), near[REACH * blocks + i, 1], preferred_element_type=jnp.float32
+        )
+        for n in range(0, 2 * listed, 2):
+            if n < listed:
+                ref, a, b = near, near_entry(i, h, n)[0], near_entry(i, h, n + 1)[0]
+            else:
+                ref, a, b = far, found_s[h, n - listed], found_s[h, n - listed + 1]
+            wa, wb = weight(n + 1), weight(n + 2)
+            total = total + (wa + wb)
+            mixed = mixed + jnp.dot(
+                jnp.concatenate([wa.astype(jnp.bfloat16), wb.astype(jnp.bfloat16)], axis=1),
+                jnp.concatenate([ref[a, 1], ref[b, 1]], axis=0),
+                preferred_element_type=jnp.float32,
+            )
+        total = jnp.sum(total, axis=1, keepdims=True)
+        rows = pl.ds(pl.multiple_of(i * BLK, BLK), BLK)
+        staged[rows, pl.ds(pl.multiple_of(h * width, width), width)] = (mixed / total).astype(jnp.bfloat16)
+
+    def full_group(ks):
+        count, before = len(ks) * heads, ks[0] * heads
+
+        def full_steps(j, carry):
+            first = 4 * j
+            for u in range(4):
+                full_scores(before + lax.rem(first + u + 2, count), (u + 2) % 4)
+                full_mix(before + first + u, u)
+            send_part(ks[0] + j // 2, j % 2)
+            return carry
+
+        for u in range(2):
+            full_scores(jnp.int32(before + u), u)
+        lax.fori_loop(0, count // 4, full_steps, 0)
+
+    for k in range(half):
         wait_input(first_query + k)
     near_group(range(half))
     for name in NAMES:
         share(name, 1 - core).wait_recv()
     share("own", 1 - core).wait_recv()
     far_group(range(half))
-    near_group(range(half, blocks))
-    far_group(range(half, blocks))
+    for k in range(half, blocks):
+        wait_input(first_query + k)
+    full_group(range(half, blocks))
 
     @pl.when(jnp.logical_not(native))
     def _():
@@ -649,12 +714,12 @@
 
     for name in NAMES:
         share(name, core).wait_send()
-        if name != "zm3":
+        if name != "zp":
             send(name).wait_send()
 
-    @pl.when(z == 1)
-    def _():
-        send("zm3").wait_send()
+    @pl.when(z == SIDE - 1)
+    def _():
+        send("zp").wait_send()
 
     share("own", core).wait_send()
 
@@ -662,18 +727,21 @@
 
         @pl.when(kept_here(k))
         def _():
-            out_keep(k).wait()
+            for c in range(2):
+                out_keep(k, c).wait()
 
         @pl.when(jnp.logical_not(kept_here(k)))
         def _():
-            out_copy(k).wait_send()
+            for c in range(2):
+                out_copy(k, c).wait_send()
 
     for of_group in range(4):
 
         @pl.when(jnp.logical_not(native & (group == of_group)))
         def _():
             for n in range(2):
-                out_in(of_group, n).wait_recv()
+                for c in range(2):
+                    out_in(of_group, n, c).wait_recv()
 
 
 def shards(queries, keys, values, vertical, slash):
@@ -688,7 +756,7 @@
     anywhere = pl.BlockSpec(memory_space=pl.ANY)
     bf16, f32 = jnp.bfloat16, jnp.float32
     inputs = 6 + blocks
-    near_width = (listed + 1) * BLK
+    full_width = (2 * listed + 1) * BLK
     return pl.pallas_call(
         functools.partial(layer_kernel, blocks=blocks, heads=heads, width=width, listed=listed),
         in_specs=[anywhere] * 5,
@@ -700,23 +768,24 @@
             pltpu.VMEM((heads, listed), jnp.int32),
             pltpu.SMEM((heads, listed), jnp.int32),
             pltpu.SMEM((2, CAP), jnp.int32),
-            pltpu.VMEM(queries.shape, bf16),
+            pltpu.VMEM((rows // 2, heads * width), bf16),
+            pltpu.VMEM((rows // 2, heads * width), bf16),
             pltpu.VMEM((blocks, 2, BLK, width), bf16),
             pltpu.VMEM((blocks, 2, BLK, width), bf16),
             pltpu.VMEM(((REACH + 1) * blocks, 2, BLK, width), bf16),
             pltpu.VMEM((2 * NODES * CAP, 2, BLK, width), bf16),
             pltpu.VMEM(queries.shape, bf16),
-            pltpu.VMEM((heads * blocks, BLK, width), f32),
-            pltpu.VMEM((heads * blocks, BLK, width), f32),
-            pltpu.VMEM((heads * blocks, BLK, width), f32),
-            pltpu.VMEM((BLK, near_width), f32),
-            pltpu.VMEM((BLK, near_width), f32),
-            pltpu.VMEM((BLK, near_width), f32),
-            pltpu.VMEM((BLK, near_width), f32),
-            pltpu.VMEM((BLK, near_width), bf16),
-            pltpu.VMEM((BLK, near_width), bf16),
-            pltpu.VMEM((BLK, near_width), bf16),
-            pltpu.VMEM((BLK, near_width), bf16),
+            pltpu.VMEM((heads * blocks // 2, BLK, width), f32),
+            pltpu.VMEM((heads * blocks // 2, BLK, width), f32),
+            pltpu.VMEM((heads * blocks // 2, BLK, width), f32),
+            pltpu.VMEM((BLK, full_width), f32),
+            pltpu.VMEM((BLK, full_width), f32),
+            pltpu.VMEM((BLK, full_width), f32),
+            pltpu.VMEM((BLK, full_width), f32),
+            pltpu.VMEM((BLK, full_width), bf16),
+            pltpu.VMEM((BLK, full_width), bf16),
+            pltpu.VMEM((BLK, full_width), bf16),
+            pltpu.VMEM((BLK, full_width), bf16),
             pltpu.VMEM((4, BLK, width), f32),
             dma((inputs,)),
             dma((inputs,)),
@@ -728,9 +797,9 @@
             dma((len(NAMES),)),
             dma((len(NAMES) + 1,)),
             dma((len(NAMES) + 1,)),
-            dma((2,)),
-            dma((blocks,)),
-            dma((2 * groups,)),
+            dma((4,)),
+            dma((2 * blocks,)),
+            dma((4 * groups,)),
         ],
         compiler_params=pltpu.CompilerParams(
             collective_id=0, has_side_effects=True, vmem_limit_bytes=62 * 1024 * 1024

time: 93.5 us -> 87.8 us (0.939); the launches traced: 93.1 us -> 86.5 us
  Pallas kernels: 88.2 us -> 81.6 us
    pallas_call x1, Pallas kernels: 88.2 us -> 81.6 us  [shards(): pl.pallas_call(functools.partial(layer_kernel, blocks=blocks, heads=heads...]
where the time goes in v4:
time: 87.8 us; the launch traced here: 86.5 us
  Pallas kernels  81.6 us (93%)
  local copies, waits for them, and re-layouts  4.92 us (6%)
    pallas_call x1, Pallas kernels, shards(): pl.pallas_call(functools.partial(layer_kernel, blocks=blocks, heads=heads...  81.6 us
    unnamed x1, local copies, waits for them, and re-layouts  3.13 us
    reshape x1, local copies, waits for them, and re-layouts, shards(): kt = jnp.swapaxes(keys.reshape(blocks, BLK, width), 1, 2)  1.79 us

profile of v4, /device:TPU:1, one launch (start us, length us, event | category | flops | bytes accessed | tf_op | source)
XLA Modules:
  0.0 86.5 jit_solution(15660085376362130213)
XLA Ops:
  0.0 1.8 %copy.6 = bf16[8,128,128]{1,2,0:T(8,128)(2,1)} copy(bf16[8,128,128]{2,1,0:T(8,128)(2,1)} %bitcast.5) | data formatting | bytes 524288 | tf_op jit(solution)/shard_map/reshape | solution.py:753
  1.8 81.6 %shard_map.55 = bf16[256,4096]{1,0:T(8,128)(2,1)} custom-call(s32[8,8]{1,0:T(8,128)} %slash_ref.1, s32[8,8]{1,0:T(8,128)} %vertical_ref.1, bf16[1024,1024]{1,0:T(8,128)(2,1)} %queries_ref.1, bf16[8,128,128]{2,1,0:T(8,128)(2,1)} %bitcast.3, bf16[8,128,128]{2,1,0:T(8,128)(2,1)} %bitcast.4), custom_call_target="tpu_custom_call" | custom-call | tf_op jit(solution)/shard_map/pallas_call | solution.py:760
  83.4 3.1 %copy.8 = bf16[256,4096]{1,0:T(8,128)(2,1)} copy(bf16[256,4096]{1,0:T(8,128)(2,1)} %shard_map.55) | data formatting | bytes 4194304

commit v5 on v4

--- a/solution.py
+++ b/solution.py
@@ -16,6 +16,7 @@
 NODES = SIDE * SIDE
 REACH = 4
 HALF = CAP // 2
+EARLY = 6
 MESH = pl.DeviceIdType.MESH
 
 COPIES = {}
@@ -49,7 +50,9 @@
 SECOND = ["zm2", "xm2", ("zmB", 1), ("xmA", 1)]
 LATER = [
     ["xp", "zp", ("xmA", 2), ("zmB", 2), ("zmB2", 1), ("xmA2", 1)],
-    [("zmB", -1), ("xmA", -1), ("xmA2", 2), ("zmB2", 2)],
+    [("zmB", -1)],
+    [("xmA", -1)],
+    [("zmB2", 2), ("xmA2", 2)],
     [("xmA2", -1), ("zmB2", -1)],
     [(name, d) for d in (1, -1, 2) for name in ("xpA", "zpB")],
 ]
@@ -59,7 +62,7 @@
     slash_ref,
     vertical_ref,
     queries_ref,
-    kt_ref,
+    k_ref,
     v_ref,
     out_ref,
     table_v,
@@ -69,6 +72,7 @@
     picked_s,
     early_q,
     late_q,
+    keys_v,
     own_ref,
     hop_ref,
     near,
@@ -138,15 +142,15 @@
     sources = [slash_ref, vertical_ref]
     targets = [table_v.at[0], table_v.at[1]]
     for c in (1, 0):
-        for kv, ref in enumerate((kt_ref, v_ref)):
-            part = pl.ds(c * half, half)
-            sources.append(ref.at[part])
-            targets.append(own_ref.at[part, kv])
+        part = pl.ds(c * half, half)
+        sources += [k_ref.at[part], v_ref.at[part]]
+        targets += [keys_v.at[part], own_ref.at[part, 1]]
     first_query = len(sources)
     for k in range(blocks):
         rows = pl.ds(pl.multiple_of(row_block(k) * BLK, BLK), BLK)
         sources.append(queries_ref.at[rows])
-        targets.append((early_q if k < half else late_q).at[pl.ds(k % half * BLK, BLK)])
+        ref, place = (early_q, k) if k < EARLY else (late_q, k - EARLY)
+        targets.append(ref.at[pl.ds(place * BLK, BLK)])
 
     def load(k):
         return pltpu.make_async_copy(sources[k], targets[k], load_sem.at[k])
@@ -337,6 +341,8 @@
     for c in (1, 0):
         for k in range(2):
             wait_input(2 + 2 * (1 - c) + k)
+        for j in range(c * half, (c + 1) * half):
+            own_ref[j, 0] = keys_v[j].T
         hop_one(c).start()
 
         @pl.when(core == 0)
@@ -427,12 +433,12 @@
     causal = lax.broadcasted_iota(jnp.int32, (BLK, BLK), 0) >= lax.broadcasted_iota(
         jnp.int32, (BLK, BLK), 1
     )
-    kept = heads * half
+    kept = heads * EARLY
     base = slab * blocks
 
     def query(ref, k, h):
         return ref[
-            pl.ds(pl.multiple_of(k % half * BLK, BLK), BLK),
+            pl.ds(pl.multiple_of(k * BLK, BLK), BLK),
             pl.ds(pl.multiple_of(h * width, width), width),
         ]
 
@@ -625,7 +631,7 @@
     def full_scores(step, u):
         k, h = step // heads, step % heads
         i = row_block(k)
-        q = query(late_q, k, h)
+        q = query(late_q, k - EARLY, h)
         own = jnp.dot(q, near[REACH * blocks + i, 0], preferred_element_type=jnp.float32)
         own = jnp.where(causal, own, NEG)
         scores[u][:, :BLK] = own
@@ -686,16 +692,16 @@
             full_scores(jnp.int32(before + u), u)
         lax.fori_loop(0, count // 4, full_steps, 0)
 
-    for k in range(half):
+    for k in range(EARLY):
         wait_input(first_query + k)
-    near_group(range(half))
+    near_group(range(EARLY))
     for name in NAMES:
         share(name, 1 - core).wait_recv()
     share("own", 1 - core).wait_recv()
-    far_group(range(half))
-    for k in range(half, blocks):
+    far_group(range(EARLY))
+    for k in range(EARLY, blocks):
         wait_input(first_query + k)
-    full_group(range(half, blocks))
+    full_group(range(EARLY, blocks))
 
     @pl.when(jnp.logical_not(native))
     def _():
@@ -750,7 +756,7 @@
     blocks = rows // BLK
     heads, listed = vertical.shape
     groups = lax.axis_size("head")
-    kt = jnp.swapaxes(keys.reshape(blocks, BLK, width), 1, 2)
+    k = keys.reshape(blocks, BLK, width)
     v = values.reshape(blocks, BLK, width)
     dma = pltpu.SemaphoreType.DMA
     anywhere = pl.BlockSpec(memory_space=pl.ANY)
@@ -768,16 +774,17 @@
             pltpu.VMEM((heads, listed), jnp.int32),
             pltpu.SMEM((heads, listed), jnp.int32),
             pltpu.SMEM((2, CAP), jnp.int32),
-            pltpu.VMEM((rows // 2, heads * width), bf16),
-            pltpu.VMEM((rows // 2, heads * width), bf16),
+            pltpu.VMEM((EARLY * BLK, heads * width), bf16),
+            pltpu.VMEM((rows - EARLY * BLK, heads * width), bf16),
+            pltpu.VMEM((blocks, BLK, width), bf16),
             pltpu.VMEM((blocks, 2, BLK, width), bf16),
             pltpu.VMEM((blocks, 2, BLK, width), bf16),
             pltpu.VMEM(((REACH + 1) * blocks, 2, BLK, width), bf16),
             pltpu.VMEM((2 * NODES * CAP, 2, BLK, width), bf16),
             pltpu.VMEM(queries.shape, bf16),
-            pltpu.VMEM((heads * blocks // 2, BLK, width), f32),
-            pltpu.VMEM((heads * blocks // 2, BLK, width), f32),
-            pltpu.VMEM((heads * blocks // 2, BLK, width), f32),
+            pltpu.VMEM((heads * EARLY, BLK, width), f32),
+            pltpu.VMEM((heads * EARLY, BLK, width), f32),
+            pltpu.VMEM((heads * EARLY, BLK, width), f32),
             pltpu.VMEM((BLK, full_width), f32),
             pltpu.VMEM((BLK, full_width), f32),
             pltpu.VMEM((BLK, full_width), f32),
@@ -804,7 +811,7 @@
         compiler_params=pltpu.CompilerParams(
             collective_id=0, has_side_effects=True, vmem_limit_bytes=62 * 1024 * 1024
         ),
-    )(slash, vertical, queries, kt, v)
+    )(slash, vertical, queries, k, v)
 
 
 def solution(mesh):

time: 87.8 us -> 84.4 us (0.961); the launches traced: 86.5 us -> 84.3 us
  local copies, waits for them, and re-layouts: 4.92 us -> 3.13 us
    reshape x1 -> x0, local copies, waits for them, and re-layouts: 1.79 us -> none  [shards(): kt = jnp.swapaxes(keys.reshape(blocks, BLK, width), 1, 2)]
where the time goes in v5:
time: 84.4 us; the launch traced here: 84.3 us
  Pallas kernels  81.2 us (96%)
  local copies, waits for them, and re-layouts  3.13 us (4%)
    pallas_call x1, Pallas kernels, shards(): pl.pallas_call(functools.partial(layer_kernel, blocks=blocks, heads=heads...  81.2 us
    unnamed x1, local copies, waits for them, and re-layouts  3.13 us

profile of v5, /device:TPU:1, one launch (start us, length us, event | category | flops | bytes accessed | tf_op | source)
XLA Modules:
  0.0 84.3 jit_solution(3945191345462170113)
XLA Ops:
  0.0 81.2 %shard_map.55 = bf16[256,4096]{1,0:T(8,128)(2,1)} custom-call(s32[8,8]{1,0:T(8,128)} %slash_ref.1, s32[8,8]{1,0:T(8,128)} %vertical_ref.1, bf16[1024,1024]{1,0:T(8,128)(2,1)} %queries_ref.1, bf16[8,128,128]{2,1,0:T(8,128)(2,1)} %bitcast.2, bf16[8,128,128]{2,1,0:T(8,128)(2,1)} %bitcast.3), custom_call_target="tpu_custom_call" | custom-call | tf_op jit(solution)/shard_map/pallas_call | solution.py:766
  81.2 3.1 %copy.7 = bf16[256,4096]{1,0:T(8,128)(2,1)} copy(bf16[256,4096]{1,0:T(8,128)(2,1)} %shard_map.55) | data formatting | bytes 4194304

commit v6 on v5

--- a/solution.py
+++ b/solution.py
@@ -53,8 +53,7 @@
     [("zmB", -1)],
     [("xmA", -1)],
     [("zmB2", 2), ("xmA2", 2)],
-    [("xmA2", -1), ("zmB2", -1)],
-    [(name, d) for d in (1, -1, 2) for name in ("xpA", "zpB")],
+    [("xmA2", -1), ("zmB2", -1)] + [(name, d) for d in (1, -1, 2) for name in ("xpA", "zpB")],
 ]
 
 
@@ -135,9 +134,9 @@
         return {"seq": 2 * node + lax.rem(of_group, 2), "head": 2 * (of_group // 2) + low}
 
     def row_block(k):
-        late = k // half
-        quarter = 2 * ((1 - late) * (1 - high) + late * high) + (k % half) // 2
-        return 2 * quarter + k % 2
+        near_turn = k % 2
+        quarter = 2 * ((1 - near_turn) * (1 - high) + near_turn * high) + k // 4
+        return 2 * quarter + k // 2 % 2
 
     sources = [slash_ref, vertical_ref]
     targets = [table_v.at[0], table_v.at[1]]
@@ -547,18 +546,18 @@
             pl.ds(pl.multiple_of(i * BLK, BLK), BLK), pl.ds(pl.multiple_of(c * part, part), part)
         ]
         first = pl.multiple_of((group * 2 + c) * part, part)
-        return here, out_ref.at[pl.ds(pl.multiple_of(k % 2 * BLK, BLK), BLK), pl.ds(first, part)]
+        return here, out_ref.at[pl.ds(pl.multiple_of(k // 2 % 2 * BLK, BLK), BLK), pl.ds(first, part)]
 
     def out_copy(k, c):
         here, there = out_refs(k, c)
         return pltpu.make_async_remote_copy(
-            here, there, out_send.at[k * 2 + c], out_recv.at[group * 4 + k % 2 * 2 + c],
+            here, there, out_send.at[k * 2 + c], out_recv.at[group * 4 + k // 2 % 2 * 2 + c],
             device_id=owner_of(row_block(k) // 2), device_id_type=MESH,
         )
 
     def out_keep(k, c):
         here, there = out_refs(k, c)
-        return pltpu.make_async_copy(here, there, out_local.at[k % 2 * 2 + c])
+        return pltpu.make_async_copy(here, there, out_local.at[k // 2 % 2 * 2 + c])
 
     def kept_here(k):
         return native & (row_block(k) // 2 == head)

time: 84.4 us -> 83.4 us (0.988)
  Pallas kernels: 81.2 us -> 80.2 us
    pallas_call x1, Pallas kernels: 81.2 us -> 80.2 us  [shards(): pl.pallas_call(functools.partial(layer_kernel, blocks=blocks, heads=heads...]
where the time goes in v6:
time: 83.4 us; the launch traced here: 83.3 us
  Pallas kernels  80.2 us (96%)
  local copies, waits for them, and re-layouts  3.13 us (4%)
    pallas_call x1, Pallas kernels, shards(): pl.pallas_call(functools.partial(layer_kernel, blocks=blocks, heads=heads...  80.2 us
    unnamed x1, local copies, waits for them, and re-layouts  3.13 us

profile of v6, /device:TPU:1, one launch (start us, length us, event | category | flops | bytes accessed | tf_op | source)
XLA Modules:
  0.0 83.3 jit_solution(13266879348394247875)
XLA Ops:
  0.0 80.2 %shard_map.55 = bf16[256,4096]{1,0:T(8,128)(2,1)} custom-call(s32[8,8]{1,0:T(8,128)} %slash_ref.1, s32[8,8]{1,0:T(8,128)} %vertical_ref.1, bf16[1024,1024]{1,0:T(8,128)(2,1)} %queries_ref.1, bf16[8,128,128]{2,1,0:T(8,128)(2,1)} %bitcast.2, bf16[8,128,128]{2,1,0:T(8,128)(2,1)} %bitcast.3), custom_call_target="tpu_custom_call" | custom-call | tf_op jit(solution)/shard_map/pallas_call | solution.py:765
  80.2 3.1 %copy.7 = bf16[256,4096]{1,0:T(8,128)(2,1)} copy(bf16[256,4096]{1,0:T(8,128)(2,1)} %shard_map.55) | data formatting | bytes 4194304

commit v7 on v6

--- a/solution.py
+++ b/solution.py
@@ -16,7 +16,7 @@
 NODES = SIDE * SIDE
 REACH = 4
 HALF = CAP // 2
-EARLY = 6
+EARLY = 5
 MESH = pl.DeviceIdType.MESH
 
 COPIES = {}

time: 83.4 us -> 82.7 us (level)
  Pallas kernels: 80.2 us -> 79.3 us
    pallas_call x1, Pallas kernels: 80.2 us -> 79.3 us  [shards(): pl.pallas_call(functools.partial(layer_kernel, blocks=blocks, heads=heads...]
where the time goes in v7:
time: 82.7 us; the launch traced here: 82.4 us
  Pallas kernels  79.3 us (96%)
  local copies, waits for them, and re-layouts  3.13 us (4%)
    pallas_call x1, Pallas kernels, shards(): pl.pallas_call(functools.partial(layer_kernel, blocks=blocks, heads=heads...  79.3 us
    unnamed x1, local copies, waits for them, and re-layouts  3.13 us

profile of v7, /device:TPU:1, one launch (start us, length us, event | category | flops | bytes accessed | tf_op | source)
XLA Modules:
  0.0 82.4 jit_solution(12704673564385618435)
XLA Ops:
  0.0 79.3 %shard_map.55 = bf16[256,4096]{1,0:T(8,128)(2,1)} custom-call(s32[8,8]{1,0:T(8,128)} %slash_ref.1, s32[8,8]{1,0:T(8,128)} %vertical_ref.1, bf16[1024,1024]{1,0:T(8,128)(2,1)} %queries_ref.1, bf16[8,128,128]{2,1,0:T(8,128)(2,1)} %bitcast.2, bf16[8,128,128]{2,1,0:T(8,128)(2,1)} %bitcast.3), custom_call_target="tpu_custom_call" | custom-call | tf_op jit(solution)/shard_map/pallas_call | solution.py:765
  79.3 3.1 %copy.7 = bf16[256,4096]{1,0:T(8,128)(2,1)} copy(bf16[256,4096]{1,0:T(8,128)(2,1)} %shard_map.55) | data formatting | bytes 4194304
